TPU v7x, 512 devices: a whole 4x4x16 slice. The times are simulated.
512 devices in a mesh: wide: 64 (over z, x), narrow: 8 (over y, core).
Axes of the slice: x: 4, y: 4, z: 16, core: 2. Of those that a mesh axis runs over, the one named last changes fastest.
Arguments:
- particle_position: float32 [3, 4096, 128], P(None, ('wide', 'narrow')), may hold values from -6 to 6
- particle_velocity: float32 [3, 4096, 128], P(None, ('wide', 'narrow')), may hold values from -6 to 6
- radius: float32 [4096, 128], P(('wide', 'narrow')), may hold values from 0.4 to 1
- block_live_count: int32 [4096], P(('wide', 'narrow')), may hold values from 64 to 128
- cell_index: int32 [4096, 128], P(('wide', 'narrow')), may hold values from 0 to 8191
- block_offset: int32 [4096], P(('wide', 'narrow')), may hold values from -2 to 2, as said below
- neighbours: int32 [4096, 6], P(('wide', 'narrow')), may hold values from 0 to 7, as said below
- gas_velocity: float32 [3, 512, 64, 128], P(None, 'wide', 'narrow'), may hold values from -6 to 6
- pressure_source: float32 [512, 64, 128], P('wide', 'narrow'), may hold values from -6 to 6
- void_before: float32 [512, 64, 128], P('wide', 'narrow'), may hold values from 0.6 to 1
Outputs:
- pressure: float32 [512, 64, 128], P('wide', 'narrow')
- gas_next: float32 [3, 512, 64, 128], P(None, 'wide', 'narrow')
- updated_particle_velocity: float32 [3, 4096, 128], P(None, ('wide', 'narrow'))
Inputs may be any that keep to these rules, and one draw needn't show every extreme that they name: For a block held at index w along wide, w + block_offset lies in 0 to 63. At most 3 blocks of one device share one offset, and on every device some offset has exactly 3. `neighbours`: each block lists 6 different blocks of its own device, never itself.
All inputs are finite; a program needn't handle non-finite values.
Results may differ from a plain program's by a relative error of at most 0.0003.
Values sent between devices are 32-bit elements; how exact they have to be, the bound alone decides.
A program may use at most 128 MiB of HBM per device.

v0:
```python
import math

import jax
import jax.numpy as jnp
from jax import lax
from jax.sharding import PartitionSpec as P

SPREAD = 2
LEVELS = 4
SWEEPS = 2
COARSE_SWEEPS = 4
CAP = 3


relax_weight = 0.8
solid_most = 0.6
void_power = 2.65
drag_base = 0.5
drag_slope = 0.5
stiffness = 16.0
softening = 0.1
particle_density = 2.0
gas_density = 1.0
step_duration = 0.25
gravity = -1.0


def extended(shard, sides, width):
    edges = {}
    for axis, dim in sides:
        size, length = (lax.axis_size(axis), shard.shape[dim])
        up = [(i, (i + 1) % size) for i in range(size - 1)]
        last = lax.slice_in_dim(shard, length - width, length, axis=dim)
        initial = lax.slice_in_dim(shard, 0, width, axis=dim)
        edges[dim] = (
            lax.ppermute(last, axis, up),
            lax.ppermute(initial, axis, [(b, a) for a, b in up]),
        )
    done = []
    for _, dim in sides:
        low, high = edges[dim]
        around = [(width, width) if d in done else (0, 0) for d in range(shard.ndim)]
        shard = jnp.concatenate([jnp.pad(low, around), shard, jnp.pad(high, around)], axis=dim)
        done.append(dim)
    return shard


def padded_2(cells, sides, width):
    for axis, dim in sides:
        count = lax.axis_size(axis)
        ends = count - 1
        head = lax.slice_in_dim(cells, 0, width, axis=dim)
        tail = lax.slice_in_dim(cells, cells.shape[dim] - width, cells.shape[dim], axis=dim)
        cells = jnp.concatenate(
            [
                lax.ppermute(tail, axis, [(i, (i + 1) % count) for i in range(ends)]),
                cells,
                lax.ppermute(head, axis, [((i + 1) % count, i) for i in range(ends)]),
            ],
            axis=dim,
        )
    return cells


def from_behind(block, axis, distance):
    devices = range(lax.axis_size(axis))
    route = [(i - distance, i) for i in devices if i - distance in devices]
    return lax.ppermute(block, axis, route)


def in_order(tiles, dim):
    tiles = jnp.moveaxis(tiles, 0, dim)
    shape = tiles.shape
    return tiles.reshape(*shape[:dim], shape[dim] * shape[dim + 1], *shape[dim + 2 :])


def from_everyone(shard, axis):
    copies = jnp.broadcast_to(shard, (lax.axis_size(axis), *shard.shape))
    return lax.all_to_all(copies, axis, split_axis=0, concat_axis=0, tiled=True)


def collect(shard, axis, dim):
    return in_order(from_everyone(shard, axis), dim)


def restrict(grid_field):
    depth_cells, lane_cells, width_cells = grid_field.shape
    return grid_field.reshape(depth_cells // 2, 2, lane_cells // 2, 2, width_cells // 2, 2).mean(
        axis=(1, 3, 5)
    )


def prolong(grid_field):
    return jnp.repeat(jnp.repeat(jnp.repeat(grid_field, 2, axis=0), 2, axis=1), 2, axis=2)


def coefs_from_padded(padded, weight):
    middle = padded[1:-1, 1:-1, 1:-1]
    couplings = (
        0.5 * weight * (middle + padded[:-2, 1:-1, 1:-1]),
        0.5 * weight * (middle + padded[2:, 1:-1, 1:-1]),
        0.5 * weight * (middle + padded[1:-1, :-2, 1:-1]),
        0.5 * weight * (middle + padded[1:-1, 2:, 1:-1]),
        0.5 * weight * (middle + padded[1:-1, 1:-1, :-2]),
        0.5 * weight * (middle + padded[1:-1, 1:-1, 2:]),
    )
    diagonal = (
        couplings[0] + couplings[1] + couplings[2] + couplings[3] + couplings[4] + couplings[5]
    )
    return (couplings, diagonal)


def apply_padded(padded, couplings, diagonal):
    middle = padded[1:-1, 1:-1, 1:-1]
    beside = couplings[0] * padded[:-2, 1:-1, 1:-1] + couplings[1] * padded[2:, 1:-1, 1:-1]
    beside = beside + couplings[2] * padded[1:-1, :-2, 1:-1] + couplings[3] * padded[1:-1, 2:, 1:-1]
    beside = beside + couplings[4] * padded[1:-1, 1:-1, :-2] + couplings[5] * padded[1:-1, 1:-1, 2:]
    return diagonal * middle - beside


def unchanged(grid_field):
    return grid_field


def pad_cells(grid_field):
    padded = extended(grid_field, (("wide", 0), ("narrow", 1)), 1)
    return jnp.pad(padded, ((0, 0), (0, 0), (1, 1)))


def pad_slab(grid_field):
    padded = padded_2(grid_field, (("wide", 0),), 1)
    return jnp.pad(padded, ((0, 0), (1, 1), (1, 1)))


def cycle(right_side, levels, level_index):
    couplings, diagonal, padder, enter_level, leave_level = levels[level_index]
    right_side = enter_level(right_side)
    coarsest = level_index == len(levels) - 1
    sweep_total = COARSE_SWEEPS if coarsest else SWEEPS
    iterate = relax_weight * right_side / diagonal
    for sweep_index in range(sweep_total - 1):
        iterate = (
            iterate
            + relax_weight
            * (right_side - apply_padded(padder(iterate), couplings, diagonal))
            / diagonal
        )
    if not coarsest:
        residual = right_side - apply_padded(padder(iterate), couplings, diagonal)
        iterate = iterate + prolong(cycle(restrict(residual), levels, level_index + 1))
        for sweep_index in range(SWEEPS):
            iterate = (
                iterate
                + relax_weight
                * (right_side - apply_padded(padder(iterate), couplings, diagonal))
                / diagonal
            )
    return leave_level(iterate)


def pressure_gradient(padded):
    return jnp.stack(
        [
            0.5 * (padded[2:, 1:-1, 1:-1] - padded[:-2, 1:-1, 1:-1]),
            0.5 * (padded[1:-1, 2:, 1:-1] - padded[1:-1, :-2, 1:-1]),
            0.5 * (padded[1:-1, 1:-1, 2:] - padded[1:-1, 1:-1, :-2]),
        ]
    )


def pairwise_force(local_positions, local_radii, local_live_mask, there_pos, there_rad, there_live):
    apart_z = local_positions[0][:, :, None] - there_pos[0][:, None, :]
    apart_y = local_positions[1][:, :, None] - there_pos[1][:, None, :]
    apart_x = local_positions[2][:, :, None] - there_pos[2][:, None, :]
    distance = jnp.sqrt(
        apart_z * apart_z + apart_y * apart_y + apart_x * apart_x + softening * softening
    )
    intersection = jnp.maximum(local_radii[:, :, None] + there_rad[:, None, :] - distance, 0.0)
    weight = intersection * there_live[:, None, :] / distance
    return local_live_mask[None] * jnp.stack(
        [
            jnp.sum(apart_z * weight, axis=2),
            jnp.sum(apart_y * weight, axis=2),
            jnp.sum(apart_x * weight, axis=2),
        ]
    )


def block_contact_forces(slot_positions, slot_radii, live_flags, adjacent_blocks):
    block_count = slot_radii.shape[0]
    batch_extent = math.gcd(block_count, 8)
    factor = stiffness / (slot_radii.shape[1] * (adjacent_blocks.shape[1] + 1))

    def one_batch(batch_index):
        total_force_sum = pairwise_force(
            slot_positions, slot_radii, live_flags, slot_positions, slot_radii, live_flags
        )
        for column in range(adjacent_blocks.shape[1]):
            selected_blocks = adjacent_blocks[:, column]
            total_force_sum = total_force_sum + pairwise_force(
                slot_positions,
                slot_radii,
                live_flags,
                slot_positions[:, selected_blocks],
                slot_radii[selected_blocks],
                live_flags[selected_blocks],
            )
        return total_force_sum * factor

    stacked = lax.map(one_batch, jnp.arange(block_count // batch_extent, dtype=jnp.int32))
    return stacked.transpose(1, 0, 2, 3).reshape(3, block_count, -1)


def local(
    particle_position,
    particle_velocity,
    radius,
    block_live_count,
    cell_index,
    block_offset,
    neighbours,
    gas_velocity,
    pressure_source,
    void_before,
):
    block_count = radius.shape[0]
    slot_count = radius.shape[1]
    depth_cells, lane_cells, width_cells = pressure_source.shape
    total_cells = depth_cells * lane_cells * width_cells
    slot_index_list = jnp.arange(slot_count, dtype=jnp.int32)
    live_flags = (slot_index_list[None, :] < block_live_count[:, None]).astype(jnp.float32)
    particle_volume = radius * radius * radius
    volume_live_mask = particle_volume * live_flags
    payload = jnp.concatenate(
        [volume_live_mask[None], particle_velocity, cell_index.astype(jnp.float32)[None]], axis=0
    )
    payload = payload.transpose(1, 0, 2).reshape(block_count, 5 * slot_count)
    block_ids = jnp.arange(block_count, dtype=jnp.int32)
    earlier = block_ids[:, None] > block_ids[None, :]
    alike = block_offset[:, None] == block_offset[None, :]
    rank_within = jnp.sum(jnp.logical_and(earlier, alike), axis=1)
    slot_key = (block_offset + SPREAD) * CAP + rank_within
    selector = (
        jnp.arange((2 * SPREAD + 1) * CAP, dtype=jnp.int32)[:, None] == slot_key[None, :]
    ).astype(jnp.float32)
    outgoing = jnp.dot(selector, payload, precision=lax.Precision.HIGHEST)
    arrived = []
    for group_index in range(2 * SPREAD + 1):
        step_by = group_index - SPREAD
        group_rows = outgoing[group_index * CAP : (group_index + 1) * CAP]
        if step_by == 0:
            arrived.append(group_rows)
        else:
            arrived.append(from_behind(group_rows, "wide", step_by))
    incoming = jnp.concatenate(arrived, axis=0)
    row_count = incoming.shape[0]
    rows_in = incoming.reshape(row_count, 5, slot_count)
    vol_in = rows_in[:, 0].reshape(-1)
    vel_in = rows_in[:, 1:4].transpose(1, 0, 2).reshape(3, -1)
    where_in = rows_in[:, 4].reshape(-1).astype(jnp.int32)
    solid_sum = jnp.zeros((total_cells,), jnp.float32).at[where_in].add(vol_in)
    voidage = 1.0 - solid_most * solid_sum / (1.0 + solid_sum)
    slip_vel = gas_velocity.reshape(3, -1)[:, where_in] - vel_in
    slip_speed = jnp.sqrt(jnp.sum(slip_vel * slip_vel, axis=0))
    drag_force = (
        vol_in * (drag_base + drag_slope * slip_speed) * voidage[where_in] ** (-void_power)
    )[None] * slip_vel
    reaction = jnp.zeros((3, total_cells), jnp.float32).at[:, where_in].add(-drag_force)
    voidage_grid = voidage.reshape(depth_cells, lane_cells, width_cells)
    right_side = pressure_source + (void_before - voidage_grid) / step_duration
    fine_levels = [voidage_grid]
    for level_index in range(1, LEVELS):
        fine_levels.append(restrict(fine_levels[-1]))
    levels = []
    far_void = collect(fine_levels[2], "narrow", 1)
    far_levels = [far_void]
    level_index = 3
    far_levels.append(restrict(far_levels[-1]))
    far_lanes = fine_levels[2].shape[1]
    far_start = lax.axis_index("narrow") * far_lanes

    def enter_far(grid_field):
        return collect(grid_field, "narrow", 1)

    def leave_far(grid_field):
        return lax.dynamic_slice_in_dim(grid_field, far_start, far_lanes, 1)

    for level_index in range(LEVELS):
        if level_index < 2:
            couplings, diagonal = coefs_from_padded(
                pad_cells(fine_levels[level_index]), 0.25**level_index
            )
            levels.append((couplings, diagonal, pad_cells, unchanged, unchanged))
        else:
            couplings, diagonal = coefs_from_padded(
                pad_slab(far_levels[level_index - 2]), 0.25**level_index
            )
            enter_level = enter_far if level_index == 2 else unchanged
            leave_level = leave_far if level_index == 2 else unchanged
            levels.append((couplings, diagonal, pad_slab, enter_level, leave_level))
    pressure = cycle(right_side, levels, 0)
    pressure_padded = extended(pressure, (("wide", 0), ("narrow", 1)), 1)
    gradient = pressure_gradient(jnp.pad(pressure_padded, ((0, 0), (0, 0), (1, 1))))
    gas_next = gas_velocity + step_duration * (
        reaction.reshape(3, depth_cells, lane_cells, width_cells)
        / (gas_density * voidage_grid)[None]
        - gradient / gas_density
    )
    fluid_force = drag_force - vol_in[None] * gradient.reshape(3, -1)[:, where_in]
    returning = (
        fluid_force.reshape(3, row_count, slot_count)
        .transpose(1, 0, 2)
        .reshape(row_count, 3 * slot_count)
    )
    back_list = []
    for group_index in range(2 * SPREAD + 1):
        step_by = group_index - SPREAD
        group_rows = returning[group_index * CAP : (group_index + 1) * CAP]
        if step_by == 0:
            back_list.append(group_rows)
        else:
            back_list.append(from_behind(group_rows, "wide", -step_by))
    returned = jnp.concatenate(back_list, axis=0)
    on_blocks = jnp.dot(selector.T, returned, precision=lax.Precision.HIGHEST)
    fluid_on = on_blocks.reshape(block_count, 3, slot_count).transpose(1, 0, 2)
    contact_force = block_contact_forces(particle_position, radius, live_flags, neighbours)
    downward = jnp.array([gravity, 0.0, 0.0], jnp.float32)[:, None, None]
    particle_acceleration = (contact_force + fluid_on) / (particle_density * particle_volume)[
        None
    ] + downward
    updated_particle_velocity = live_flags[None] * (
        particle_velocity + step_duration * particle_acceleration
    )
    return (pressure, gas_next, updated_particle_velocity)


def solution(mesh):
    placed = (
        P(None, ("wide", "narrow"), None),
        P(None, ("wide", "narrow"), None),
        P(("wide", "narrow"), None),
        P(("wide", "narrow")),
        P(("wide", "narrow"), None),
        P(("wide", "narrow")),
        P(("wide", "narrow"), None),
        P(None, "wide", "narrow", None),
        P("wide", "narrow", None),
        P("wide", "narrow", None),
    )
    return jax.shard_map(
        local,
        mesh=mesh,
        in_specs=placed,
        out_specs=(
            P("wide", "narrow", None),
            P(None, "wide", "narrow", None),
            P(None, ("wide", "narrow"), None),
        ),
        check_vma=False,
    )
```

profile of v0, /device:TPU:108, one launch (start us, length us, event | category | flops | bytes accessed | tf_op | source)
XLA Modules:
  0.0 405.9 jit_solution(11685310054666606068)
XLA Ops:
  7.0 3.6 collective-permute-start.1
  12.9 7.0 %collective-permute-start.3 = (f32[3,640]{1,0:T(4,128)S(1)}, f32[3,640]{1,0:T(4,128)S(1)}, u32[]{:S(2)}, u32[]{:S(2)}) collective-permute-start(f32[3,640]{1,0:T(4,128)S(1)} %get-tuple-element.91), channel_id=1, source_target_pairs={{0,16},{8,24},{16,32},{24,40},{32,48},{40,56},{48,64},{56,72},{64,... | collective-permute-start | bytes 23048 | tf_op jit(solution)/shard_map/ppermute | solution.py:68
  33.1 3.8 fusion.36
  38.5 12.6 %scatter_custom_fusion = f32[8192]{0:T(1024)S(1)} fusion(s32[1920]{0:T(1024)S(1)} %fusion.266, f32[1920]{0:T(1024)S(1)} %bitcast.267, f32[]{:T(128)} %constant.24.clone.1), kind=kCustom, calls=%fused_computation.441 | custom fusion | flops 1920 | bytes 32772 | tf_op jit(solution)/shard_map/scatter-add | solution.py:261
  55.1 3.6 collective-permute-start.7
  67.2 3.6 collective-permute-start.19
  83.4 5.5 %all-to-all-start.1 = ((f32[8,1,128]{2,1,0:T(1,128)}), f32[8,1,128]{2,1,0:T(1,128)S(1)}, u32[]{:S(2)}, u32[]{:S(2)}) async-start(f32[8,1,128]{2,1,0:T(1,128)} %reshape.510), calls=%async_computation.1 | async-start | bytes 8192 | tf_op jit(solution)/shard_map/all_to_all | solution.py:79
  89.0 5.5 %collective-permute-start.16 = (f32[1,4,64]{2,1,0:T(4,128)S(1)}, f32[1,4,64]{2,1,0:T(4,128)S(1)}, u32[]{:S(2)}, u32[]{:S(2)}) collective-permute-start(f32[1,4,64]{2,1,0:T(4,128)S(1)} %get-tuple-element.177), channel_id=1, source_target_pairs={{0,8},{8,16},{16,24},{24,32},{32,40},{40,48},{48,56},{56,64},{64,7... | collective-permute-start | bytes 3080 | tf_op jit(solution)/shard_map/ppermute | solution.py:36
  98.7 3.6 collective-permute-start.15
  102.3 7.2 %collective-permute-start.12 = (f32[1,8,128]{2,1,0:T(8,128)S(1)}, f32[1,8,128]{2,1,0:T(8,128)S(1)}, u32[]{:S(2)}, u32[]{:S(2)}) collective-permute-start(f32[1,8,128]{2,1,0:T(8,128)S(1)} %get-tuple-element.108), channel_id=1, source_target_pairs={{0,8},{8,16},{16,24},{24,32},{32,40},{40,48},{48,56},{56,64},{64,7... | collective-permute-start | bytes 12296 | tf_op jit(solution)/shard_map/ppermute | solution.py:36
  113.0 5.5 %collective-permute-done.13 = f32[1,8,128]{2,1,0:T(8,128)S(1)} collective-permute-done((f32[1,8,128]{2,1,0:T(8,128)S(1)}, f32[1,8,128]{2,1,0:T(8,128)S(1)}, u32[]{:S(2)}, u32[]{:S(2)}) %collective-permute-start.13) | collective-permute-done | bytes 4128 | tf_op jit(solution)/shard_map/ppermute | solution.py:37
  123.1 3.6 collective-permute-start.23
  126.7 7.2 %collective-permute-start.20 = (f32[1,4,64]{2,1,0:T(4,128)S(1)}, f32[1,4,64]{2,1,0:T(4,128)S(1)}, u32[]{:S(2)}, u32[]{:S(2)}) collective-permute-start(f32[1,4,64]{2,1,0:T(4,128)S(1)} %get-tuple-element.170), channel_id=1, source_target_pairs={{0,8},{8,16},{16,24},{24,32},{32,40},{40,48},{48,56},{56,64},{64,7... | collective-permute-start | bytes 3080 | tf_op jit(solution)/shard_map/ppermute | solution.py:36
  136.0 3.5 collective-permute-done.21
  141.6 3.6 collective-permute-start.27
  145.2 5.2 %collective-permute-start.24 = (f32[1,4,64]{2,1,0:T(4,128)S(1)}, f32[1,4,64]{2,1,0:T(4,128)S(1)}, u32[]{:S(2)}, u32[]{:S(2)}) collective-permute-start(f32[1,4,64]{2,1,0:T(4,128)S(1)} %get-tuple-element.166), channel_id=1, source_target_pairs={{0,8},{8,16},{16,24},{24,32},{32,40},{40,48},{48,56},{56,64},{64,7... | collective-permute-start | bytes 3080 | tf_op jit(solution)/shard_map/ppermute | solution.py:36
  152.4 3.9 collective-permute-start.28
  159.8 4.8 %all-to-all-start = ((f32[8,1,128]{2,1,0:T(1,128)}), f32[8,1,128]{2,1,0:T(1,128)S(1)}, u32[]{:S(2)}, u32[]{:S(2)}) async-start(f32[8,1,128]{2,1,0:T(1,128)} %reshape.512), calls=%async_computation | async-start | bytes 8192 | tf_op jit(solution)/shard_map/all_to_all | solution.py:79
  164.7 3.7 all-to-all-done
  169.2 5.2 %collective-permute-start.30 = (f32[1,16,32]{2,1,0:T(8,128)S(1)}, f32[1,16,32]{2,1,0:T(8,128)S(1)}, u32[]{:S(2)}, u32[]{:S(2)}) collective-permute-start(f32[1,16,32]{2,1,0:T(8,128)S(1)} %get-tuple-element.133), channel_id=1, source_target_pairs={{0,8},{8,16},{16,24},{24,32},{32,40},{40,48},{48,56},{56,64},{64,7... | collective-permute-start | bytes 6152 | tf_op jit(solution)/shard_map/ppermute | solution.py:56
  176.4 7.2 %collective-permute-start.34 = (f32[1,8,16]{2,1,0:T(8,128)S(1)}, f32[1,8,16]{2,1,0:T(8,128)S(1)}, u32[]{:S(2)}, u32[]{:S(2)}) collective-permute-start(f32[1,8,16]{2,1,0:T(8,128)S(1)} %multiply_bitcast_fusion), channel_id=1, source_target_pairs={{0,8},{8,16},{16,24},{24,32},{32,40},{40,48},{48,56},{56,64},{64,7... | collective-permute-start | bytes 1544 | tf_op jit(solution)/shard_map/ppermute | solution.py:56
  185.8 7.2 %collective-permute-start.32 = (f32[1,16,32]{2,1,0:T(8,128)S(1)}, f32[1,16,32]{2,1,0:T(8,128)S(1)}, u32[]{:S(2)}, u32[]{:S(2)}) collective-permute-start(f32[1,16,32]{2,1,0:T(8,128)S(1)} %get-tuple-element.131), channel_id=1, source_target_pairs={{0,8},{8,16},{16,24},{24,32},{32,40},{40,48},{48,56},{56,64},{64,7... | collective-permute-start | bytes 6152 | tf_op jit(solution)/shard_map/ppermute | solution.py:56
  195.1 6.8 %collective-permute-done.33 = f32[1,16,32]{2,1,0:T(8,128)S(1)} collective-permute-done((f32[1,16,32]{2,1,0:T(8,128)S(1)}, f32[1,16,32]{2,1,0:T(8,128)S(1)}, u32[]{:S(2)}, u32[]{:S(2)}) %collective-permute-start.33) | collective-permute-done | bytes 2080 | tf_op jit(solution)/shard_map/ppermute | solution.py:58
  202.4 7.2 %collective-permute-start.36 = (f32[1,8,16]{2,1,0:T(8,128)S(1)}, f32[1,8,16]{2,1,0:T(8,128)S(1)}, u32[]{:S(2)}, u32[]{:S(2)}) collective-permute-start(f32[1,8,16]{2,1,0:T(8,128)S(1)} %get-tuple-element.63), channel_id=1, source_target_pairs={{0,8},{8,16},{16,24},{24,32},{32,40},{40,48},{48,56},{56,64},{64,7... | collective-permute-start | bytes 1544 | tf_op jit(solution)/shard_map/ppermute | solution.py:56
  215.3 5.2 %collective-permute-start.38 = (f32[1,8,16]{2,1,0:T(8,128)S(1)}, f32[1,8,16]{2,1,0:T(8,128)S(1)}, u32[]{:S(2)}, u32[]{:S(2)}) collective-permute-start(f32[1,8,16]{2,1,0:T(8,128)S(1)} %fusion.298), channel_id=1, source_target_pairs={{0,8},{8,16},{16,24},{24,32},{32,40},{40,48},{48,56},{56,64},{64,7... | collective-permute-start | bytes 1544 | tf_op jit(solution)/shard_map/ppermute | solution.py:56
  226.2 5.2 %collective-permute-start.40 = (f32[1,8,16]{2,1,0:T(8,128)S(1)}, f32[1,8,16]{2,1,0:T(8,128)S(1)}, u32[]{:S(2)}, u32[]{:S(2)}) collective-permute-start(f32[1,8,16]{2,1,0:T(8,128)S(1)} %fusion.289), channel_id=1, source_target_pairs={{0,8},{8,16},{16,24},{24,32},{32,40},{40,48},{48,56},{56,64},{64,7... | collective-permute-start | bytes 1544 | tf_op jit(solution)/shard_map/ppermute | solution.py:56
  237.5 7.1 %collective-permute-start.42 = (f32[1,16,32]{2,1,0:T(8,128)S(1)}, f32[1,16,32]{2,1,0:T(8,128)S(1)}, u32[]{:S(2)}, u32[]{:S(2)}) collective-permute-start(f32[1,16,32]{2,1,0:T(8,128)S(1)} %get-tuple-element.129), channel_id=1, source_target_pairs={{0,8},{8,16},{16,24},{24,32},{32,40},{40,48},{48,56},{56,64},{64,7... | collective-permute-start | bytes 6152 | tf_op jit(solution)/shard_map/ppermute | solution.py:56
  250.6 6.4 %collective-permute-start.44 = (f32[1,16,32]{2,1,0:T(8,128)S(1)}, f32[1,16,32]{2,1,0:T(8,128)S(1)}, u32[]{:S(2)}, u32[]{:S(2)}) collective-permute-start(f32[1,16,32]{2,1,0:T(8,128)S(1)} %get-tuple-element.127), channel_id=1, source_target_pairs={{0,8},{8,16},{16,24},{24,32},{32,40},{40,48},{48,56},{56,64},{64,7... | collective-permute-start | bytes 6152 | tf_op jit(solution)/shard_map/ppermute | solution.py:56
  258.9 3.9 collective-permute-done.45
  265.3 3.6 collective-permute-start.49
  268.9 7.2 %collective-permute-start.46 = (f32[1,4,64]{2,1,0:T(4,128)S(1)}, f32[1,4,64]{2,1,0:T(4,128)S(1)}, u32[]{:S(2)}, u32[]{:S(2)}) collective-permute-start(f32[1,4,64]{2,1,0:T(4,128)S(1)} %get-tuple-element.162), channel_id=1, source_target_pairs={{0,8},{8,16},{16,24},{24,32},{32,40},{40,48},{48,56},{56,64},{64,7... | collective-permute-start | bytes 3080 | tf_op jit(solution)/shard_map/ppermute | solution.py:36
  278.1 5.7 %gather_fusion = f32[1920,3]{1,0:T(8,128)S(1)} fusion(f32[3,8192]{0,1:T(8,128)} %bitcast.231, s32[2048]{0:T(1024)S(1)} %pad_clamp_fusion), kind=kCustom, calls=%fused_computation | custom fusion | bytes 53760 | tf_op jit(solution)/shard_map/gather | solution.py:263
  286.3 3.6 collective-permute-start.53
  290.0 3.9 collective-permute-start.50
  295.9 10.4 %gather_fusion.1 = f32[1920]{0:T(1024)S(1)} fusion(f32[8192]{0:T(1024)S(1)} %get-tuple-element.120, s32[2048]{0:T(1024)S(1)} %pad_clamp_fusion), kind=kCustom, calls=%fused_computation.1 | custom fusion | bytes 23040 | tf_op jit(solution)/shard_map/gather | solution.py:266
  308.9 3.6 collective-permute-start.57
  312.6 5.2 %collective-permute-start.54 = (f32[1,8,128]{2,1,0:T(8,128)S(1)}, f32[1,8,128]{2,1,0:T(8,128)S(1)}, u32[]{:S(2)}, u32[]{:S(2)}) collective-permute-start(f32[1,8,128]{2,1,0:T(8,128)S(1)} %get-tuple-element.104), channel_id=1, source_target_pairs={{0,8},{8,16},{16,24},{24,32},{32,40},{40,48},{48,56},{56,64},{64,7... | collective-permute-start | bytes 12296 | tf_op jit(solution)/shard_map/ppermute | solution.py:36
  320.2 6.4 %collective-permute-done.55 = f32[1,8,128]{2,1,0:T(8,128)S(1)} collective-permute-done((f32[1,8,128]{2,1,0:T(8,128)S(1)}, f32[1,8,128]{2,1,0:T(8,128)S(1)}, u32[]{:S(2)}, u32[]{:S(2)}) %collective-permute-start.55) | collective-permute-done | bytes 4128 | tf_op jit(solution)/shard_map/ppermute | solution.py:37
  328.9 3.6 collective-permute-start.61
  332.5 7.2 %collective-permute-start.58 = (f32[1,8,128]{2,1,0:T(8,128)S(1)}, f32[1,8,128]{2,1,0:T(8,128)S(1)}, u32[]{:S(2)}, u32[]{:S(2)}) collective-permute-start(f32[1,8,128]{2,1,0:T(8,128)S(1)} %get-tuple-element.100), channel_id=1, source_target_pairs={{0,8},{8,16},{16,24},{24,32},{32,40},{40,48},{48,56},{56,64},{64,7... | collective-permute-start | bytes 12296 | tf_op jit(solution)/shard_map/ppermute | solution.py:36
  342.1 3.2 collective-permute-done.59
  351.8 5.2 %collective-permute-start.63 = (f32[1,8,128]{2,1,0:T(8,128)S(1)}, f32[1,8,128]{2,1,0:T(8,128)S(1)}, u32[]{:S(2)}, u32[]{:S(2)}) collective-permute-start(f32[1,8,128]{2,1,0:T(8,128)S(1)} %get-tuple-element.96), channel_id=1, source_target_pairs={{0,8},{8,16},{16,24},{24,32},{32,40},{40,48},{48,56},{56,64},{64,7... | collective-permute-start | bytes 12296 | tf_op jit(solution)/shard_map/ppermute | solution.py:36
  357.1 14.2 %scatter_custom_fusion.1 = f32[3,8192]{0,1:T(8,128)} fusion(s32[1920]{0:T(1024)S(1)} %fusion.266, f32[]{:T(128)} %constant.24.clone.1, f32[3,1920]{0,1:T(8,128)S(1)} %fusion.10), kind=kCustom, calls=%fused_computation.23 | custom fusion | flops 5760 | bytes 1081348 | tf_op jit(solution)/shard_map/scatter-add | solution.py:268
  377.3 5.7 %gather_fusion.20 = f32[1920,3]{1,0:T(8,128)S(1)} fusion(f32[3,8192]{0,1:T(8,128)} %copy.170, s32[2048]{0:T(1024)S(1)} %pad_clamp_fusion), kind=kCustom, calls=%fused_computation.20 | custom fusion | bytes 53760 | tf_op jit(solution)/shard_map/gather | solution.py:309
  383.4 6.4 %collective-permute-start.66 = (f32[3,384]{1,0:T(4,128)S(1)}, f32[3,384]{1,0:T(4,128)S(1)}, u32[]{:S(2)}, u32[]{:S(2)}) collective-permute-start(f32[3,384]{1,0:T(4,128)S(1)} %bitcast.273), channel_id=1, source_target_pairs={{0,16},{8,24},{16,32},{24,40},{32,48},{40,56},{48,64},{56,72},{64,... | collective-permute-start | bytes 13832 | tf_op jit(solution)/shard_map/ppermute | solution.py:68
  392.3 3.4 collective-permute-start.68
  395.7 3.4 collective-permute-start.69
  399.8 5.1 %collective-permute-done.69 = f32[3,384]{1,0:T(4,128)S(1)} collective-permute-done((f32[3,384]{1,0:T(4,128)S(1)}, f32[3,384]{1,0:T(4,128)S(1)}, u32[]{:S(2)}, u32[]{:S(2)}) %collective-permute-start.69) | collective-permute-done | bytes 4640 | tf_op jit(solution)/shard_map/ppermute | solution.py:68
  (324 shorter events, 137.1 us)
Async XLA Ops:
  4.5 33.6 %collective-permute-start = (f32[3,640]{1,0:T(4,128)S(1)}, f32[3,640]{1,0:T(4,128)S(1)}, u32[]{:S(2)}, u32[]{:S(2)}) collective-permute-start(f32[3,640]{1,0:T(4,128)S(1)} %get-tuple-element.95), channel_id=1, source_target_pairs={{16,0},{24,8},{32,16},{40,24},{48,32},{56,40},{64,48},{72,56},{80,... | collective-permute-start | bytes 23048 | tf_op jit(solution)/shard_map/ppermute | solution.py:68
  7.0 31.2 %collective-permute-start.1 = (f32[3,640]{1,0:T(4,128)S(1)}, f32[3,640]{1,0:T(4,128)S(1)}, u32[]{:S(2)}, u32[]{:S(2)}) collective-permute-start(f32[3,640]{1,0:T(4,128)S(1)} %get-tuple-element.94), channel_id=1, source_target_pairs={{8,0},{16,8},{24,16},{32,24},{40,32},{48,40},{56,48},{64,56},{72,6... | collective-permute-start | bytes 23048 | tf_op jit(solution)/shard_map/ppermute | solution.py:68
  10.6 27.6 %collective-permute-start.2 = (f32[3,640]{1,0:T(4,128)S(1)}, f32[3,640]{1,0:T(4,128)S(1)}, u32[]{:S(2)}, u32[]{:S(2)}) collective-permute-start(f32[3,640]{1,0:T(4,128)S(1)} %get-tuple-element.92), channel_id=1, source_target_pairs={{0,8},{8,16},{16,24},{24,32},{32,40},{40,48},{48,56},{56,64},{64,7... | collective-permute-start | bytes 23048 | tf_op jit(solution)/shard_map/ppermute | solution.py:68
  12.9 25.3 %collective-permute-start.3 = (f32[3,640]{1,0:T(4,128)S(1)}, f32[3,640]{1,0:T(4,128)S(1)}, u32[]{:S(2)}, u32[]{:S(2)}) collective-permute-start(f32[3,640]{1,0:T(4,128)S(1)} %get-tuple-element.91), channel_id=1, source_target_pairs={{0,16},{8,24},{16,32},{24,40},{32,48},{40,56},{48,64},{56,72},{64,... | collective-permute-start | bytes 23048 | tf_op jit(solution)/shard_map/ppermute | solution.py:68
  53.2 14.0 %collective-permute-start.6 = (f32[8,1,128]{2,1,0:T(1,128)S(1)}, f32[8,1,128]{2,1,0:T(1,128)S(1)}, u32[]{:S(2)}, u32[]{:S(2)}) collective-permute-start(f32[8,1,128]{2,1,0:T(1,128)S(1)} %get-tuple-element.117), channel_id=1, source_target_pairs={{0,1},{1,2},{2,3},{3,4},{4,5},{5,6},{6,7},{8,9},{9,10},{10,11},{11... | collective-permute-start | bytes 12296 | tf_op jit(solution)/shard_map/ppermute | solution.py:36
  55.1 15.8 %collective-permute-start.7 = (f32[8,1,128]{2,1,0:T(1,128)S(1)}, f32[8,1,128]{2,1,0:T(1,128)S(1)}, u32[]{:S(2)}, u32[]{:S(2)}) collective-permute-start(f32[8,1,128]{2,1,0:T(1,128)S(1)} %get-tuple-element.116), channel_id=1, source_target_pairs={{1,0},{2,1},{3,2},{4,3},{5,4},{6,5},{7,6},{9,8},{10,9},{11,10},{12... | collective-permute-start | bytes 12296 | tf_op jit(solution)/shard_map/ppermute | solution.py:37
  58.8 12.1 %collective-permute-start.4 = (f32[1,8,128]{2,1,0:T(8,128)S(1)}, f32[1,8,128]{2,1,0:T(8,128)S(1)}, u32[]{:S(2)}, u32[]{:S(2)}) collective-permute-start(f32[1,8,128]{2,1,0:T(8,128)S(1)} %get-tuple-element.119), channel_id=1, source_target_pairs={{0,8},{8,16},{16,24},{24,32},{32,40},{40,48},{48,56},{56,64},{64,7... | collective-permute-start | bytes 12296 | tf_op jit(solution)/shard_map/ppermute | solution.py:36
  65.2 14.6 %collective-permute-start.18 = (f32[4,1,64]{2,1,0:T(1,128)S(1)}, f32[4,1,64]{2,1,0:T(1,128)S(1)}, u32[]{:S(2)}, u32[]{:S(2)}) collective-permute-start(f32[4,1,64]{2,1,0:T(1,128)S(1)} %get-tuple-element.175), channel_id=1, source_target_pairs={{0,1},{1,2},{2,3},{3,4},{4,5},{5,6},{6,7},{8,9},{9,10},{10,11},{11... | collective-permute-start | bytes 3080 | tf_op jit(solution)/shard_map/ppermute | solution.py:36
  67.2 21.7 %collective-permute-start.19 = (f32[4,1,64]{2,1,0:T(1,128)S(1)}, f32[4,1,64]{2,1,0:T(1,128)S(1)}, u32[]{:S(2)}, u32[]{:S(2)}) collective-permute-start(f32[4,1,64]{2,1,0:T(1,128)S(1)} %get-tuple-element.174), channel_id=1, source_target_pairs={{1,0},{2,1},{3,2},{4,3},{5,4},{6,5},{7,6},{9,8},{10,9},{11,10},{12... | collective-permute-start | bytes 3080 | tf_op jit(solution)/shard_map/ppermute | solution.py:37
  71.3 23.2 %collective-permute-start.10 = (f32[8,1,128]{2,1,0:T(1,128)S(1)}, f32[8,1,128]{2,1,0:T(1,128)S(1)}, u32[]{:S(2)}, u32[]{:S(2)}) collective-permute-start(f32[8,1,128]{2,1,0:T(1,128)S(1)} %get-tuple-element.114), channel_id=1, source_target_pairs={{0,1},{1,2},{2,3},{3,4},{4,5},{5,6},{6,7},{8,9},{9,10},{10,11},{11... | collective-permute-start | bytes 12296 | tf_op jit(solution)/shard_map/ppermute | solution.py:36
  73.8 22.7 %collective-permute-start.11 = (f32[8,1,128]{2,1,0:T(1,128)S(1)}, f32[8,1,128]{2,1,0:T(1,128)S(1)}, u32[]{:S(2)}, u32[]{:S(2)}) collective-permute-start(f32[8,1,128]{2,1,0:T(1,128)S(1)} %get-tuple-element.115), channel_id=1, source_target_pairs={{1,0},{2,1},{3,2},{4,3},{5,4},{6,5},{7,6},{9,8},{10,9},{11,10},{12... | collective-permute-start | bytes 12296 | tf_op jit(solution)/shard_map/ppermute | solution.py:37
  76.8 19.6 %collective-permute-start.8 = (f32[1,8,128]{2,1,0:T(8,128)S(1)}, f32[1,8,128]{2,1,0:T(8,128)S(1)}, u32[]{:S(2)}, u32[]{:S(2)}) collective-permute-start(f32[1,8,128]{2,1,0:T(8,128)S(1)} %get-tuple-element.112), channel_id=1, source_target_pairs={{0,8},{8,16},{16,24},{24,32},{32,40},{40,48},{48,56},{56,64},{64,7... | collective-permute-start | bytes 12296 | tf_op jit(solution)/shard_map/ppermute | solution.py:36
  79.8 16.7 %collective-permute-start.9 = (f32[1,8,128]{2,1,0:T(8,128)S(1)}, f32[1,8,128]{2,1,0:T(8,128)S(1)}, u32[]{:S(2)}, u32[]{:S(2)}) collective-permute-start(f32[1,8,128]{2,1,0:T(8,128)S(1)} %get-tuple-element.113), channel_id=1, source_target_pairs={{8,0},{16,8},{24,16},{32,24},{40,32},{48,40},{56,48},{64,56},{72,6... | collective-permute-start | bytes 12296 | tf_op jit(solution)/shard_map/ppermute | solution.py:37
  83.4 28.2 %all-to-all-start.1 = ((f32[8,1,128]{2,1,0:T(1,128)}), f32[8,1,128]{2,1,0:T(1,128)S(1)}, u32[]{:S(2)}, u32[]{:S(2)}) async-start(f32[8,1,128]{2,1,0:T(1,128)} %reshape.510), calls=%async_computation.1 | async-start | bytes 8192 | tf_op jit(solution)/shard_map/all_to_all | solution.py:79
  89.0 20.6 %collective-permute-start.16 = (f32[1,4,64]{2,1,0:T(4,128)S(1)}, f32[1,4,64]{2,1,0:T(4,128)S(1)}, u32[]{:S(2)}, u32[]{:S(2)}) collective-permute-start(f32[1,4,64]{2,1,0:T(4,128)S(1)} %get-tuple-element.177), channel_id=1, source_target_pairs={{0,8},{8,16},{16,24},{24,32},{32,40},{40,48},{48,56},{56,64},{64,7... | collective-permute-start | bytes 3080 | tf_op jit(solution)/shard_map/ppermute | solution.py:36
  94.5 17.1 %collective-permute-start.17 = (f32[1,4,64]{2,1,0:T(4,128)S(1)}, f32[1,4,64]{2,1,0:T(4,128)S(1)}, u32[]{:S(2)}, u32[]{:S(2)}) collective-permute-start(f32[1,4,64]{2,1,0:T(4,128)S(1)} %get-tuple-element.176), channel_id=1, source_target_pairs={{8,0},{16,8},{24,16},{32,24},{40,32},{48,40},{56,48},{64,56},{72,6... | collective-permute-start | bytes 3080 | tf_op jit(solution)/shard_map/ppermute | solution.py:37
  96.8 16.1 %collective-permute-start.14 = (f32[8,1,128]{2,1,0:T(1,128)S(1)}, f32[8,1,128]{2,1,0:T(1,128)S(1)}, u32[]{:S(2)}, u32[]{:S(2)}) collective-permute-start(f32[8,1,128]{2,1,0:T(1,128)S(1)} %get-tuple-element.110), channel_id=1, source_target_pairs={{0,1},{1,2},{2,3},{3,4},{4,5},{5,6},{6,7},{8,9},{9,10},{10,11},{11... | collective-permute-start | bytes 12296 | tf_op jit(solution)/shard_map/ppermute | solution.py:36
  98.7 14.2 %collective-permute-start.15 = (f32[8,1,128]{2,1,0:T(1,128)S(1)}, f32[8,1,128]{2,1,0:T(1,128)S(1)}, u32[]{:S(2)}, u32[]{:S(2)}) collective-permute-start(f32[8,1,128]{2,1,0:T(1,128)S(1)} %get-tuple-element.111), channel_id=1, source_target_pairs={{1,0},{2,1},{3,2},{4,3},{5,4},{6,5},{7,6},{9,8},{10,9},{11,10},{12... | collective-permute-start | bytes 12296 | tf_op jit(solution)/shard_map/ppermute | solution.py:37
  102.3 10.6 %collective-permute-start.12 = (f32[1,8,128]{2,1,0:T(8,128)S(1)}, f32[1,8,128]{2,1,0:T(8,128)S(1)}, u32[]{:S(2)}, u32[]{:S(2)}) collective-permute-start(f32[1,8,128]{2,1,0:T(8,128)S(1)} %get-tuple-element.108), channel_id=1, source_target_pairs={{0,8},{8,16},{16,24},{24,32},{32,40},{40,48},{48,56},{56,64},{64,7... | collective-permute-start | bytes 12296 | tf_op jit(solution)/shard_map/ppermute | solution.py:36
  121.1 14.8 %collective-permute-start.22 = (f32[4,1,64]{2,1,0:T(1,128)S(1)}, f32[4,1,64]{2,1,0:T(1,128)S(1)}, u32[]{:S(2)}, u32[]{:S(2)}) collective-permute-start(f32[4,1,64]{2,1,0:T(1,128)S(1)} %get-tuple-element.172), channel_id=1, source_target_pairs={{0,1},{1,2},{2,3},{3,4},{4,5},{5,6},{6,7},{8,9},{9,10},{10,11},{11... | collective-permute-start | bytes 3080 | tf_op jit(solution)/shard_map/ppermute | solution.py:36
  123.1 12.9 %collective-permute-start.23 = (f32[4,1,64]{2,1,0:T(1,128)S(1)}, f32[4,1,64]{2,1,0:T(1,128)S(1)}, u32[]{:S(2)}, u32[]{:S(2)}) collective-permute-start(f32[4,1,64]{2,1,0:T(1,128)S(1)} %get-tuple-element.173), channel_id=1, source_target_pairs={{1,0},{2,1},{3,2},{4,3},{5,4},{6,5},{7,6},{9,8},{10,9},{11,10},{12... | collective-permute-start | bytes 3080 | tf_op jit(solution)/shard_map/ppermute | solution.py:37
  139.6 16.9 %collective-permute-start.26 = (f32[4,1,64]{2,1,0:T(1,128)S(1)}, f32[4,1,64]{2,1,0:T(1,128)S(1)}, u32[]{:S(2)}, u32[]{:S(2)}) collective-permute-start(f32[4,1,64]{2,1,0:T(1,128)S(1)} %get-tuple-element.168), channel_id=1, source_target_pairs={{0,1},{1,2},{2,3},{3,4},{4,5},{5,6},{6,7},{8,9},{9,10},{10,11},{11... | collective-permute-start | bytes 3080 | tf_op jit(solution)/shard_map/ppermute | solution.py:36
  141.6 16.9 %collective-permute-start.27 = (f32[4,1,64]{2,1,0:T(1,128)S(1)}, f32[4,1,64]{2,1,0:T(1,128)S(1)}, u32[]{:S(2)}, u32[]{:S(2)}) collective-permute-start(f32[4,1,64]{2,1,0:T(1,128)S(1)} %get-tuple-element.169), channel_id=1, source_target_pairs={{1,0},{2,1},{3,2},{4,3},{5,4},{6,5},{7,6},{9,8},{10,9},{11,10},{12... | collective-permute-start | bytes 3080 | tf_op jit(solution)/shard_map/ppermute | solution.py:37
  145.2 13.3 %collective-permute-start.24 = (f32[1,4,64]{2,1,0:T(4,128)S(1)}, f32[1,4,64]{2,1,0:T(4,128)S(1)}, u32[]{:S(2)}, u32[]{:S(2)}) collective-permute-start(f32[1,4,64]{2,1,0:T(4,128)S(1)} %get-tuple-element.166), channel_id=1, source_target_pairs={{0,8},{8,16},{16,24},{24,32},{32,40},{40,48},{48,56},{56,64},{64,7... | collective-permute-start | bytes 3080 | tf_op jit(solution)/shard_map/ppermute | solution.py:36
  152.4 12.2 %collective-permute-start.28 = (f32[1,16,32]{2,1,0:T(8,128)S(1)}, f32[1,16,32]{2,1,0:T(8,128)S(1)}, u32[]{:S(2)}, u32[]{:S(2)}) collective-permute-start(f32[1,16,32]{2,1,0:T(8,128)S(1)} %bitcast.272), channel_id=1, source_target_pairs={{0,8},{8,16},{16,24},{24,32},{32,40},{40,48},{48,56},{56,64},{64,7... | collective-permute-start | bytes 6152 | tf_op jit(solution)/shard_map/ppermute | solution.py:56
  169.2 16.4 %collective-permute-start.30 = (f32[1,16,32]{2,1,0:T(8,128)S(1)}, f32[1,16,32]{2,1,0:T(8,128)S(1)}, u32[]{:S(2)}, u32[]{:S(2)}) collective-permute-start(f32[1,16,32]{2,1,0:T(8,128)S(1)} %get-tuple-element.133), channel_id=1, source_target_pairs={{0,8},{8,16},{16,24},{24,32},{32,40},{40,48},{48,56},{56,64},{64,7... | collective-permute-start | bytes 6152 | tf_op jit(solution)/shard_map/ppermute | solution.py:56
  174.5 11.1 %collective-permute-start.31 = (f32[1,16,32]{2,1,0:T(8,128)S(1)}, f32[1,16,32]{2,1,0:T(8,128)S(1)}, u32[]{:S(2)}, u32[]{:S(2)}) collective-permute-start(f32[1,16,32]{2,1,0:T(8,128)S(1)} %get-tuple-element.134), channel_id=1, source_target_pairs={{8,0},{16,8},{24,16},{32,24},{40,32},{48,40},{56,48},{64,56},{72,6... | collective-permute-start | bytes 6152 | tf_op jit(solution)/shard_map/ppermute | solution.py:58
  176.4 18.6 %collective-permute-start.34 = (f32[1,8,16]{2,1,0:T(8,128)S(1)}, f32[1,8,16]{2,1,0:T(8,128)S(1)}, u32[]{:S(2)}, u32[]{:S(2)}) collective-permute-start(f32[1,8,16]{2,1,0:T(8,128)S(1)} %multiply_bitcast_fusion), channel_id=1, source_target_pairs={{0,8},{8,16},{16,24},{24,32},{32,40},{40,48},{48,56},{56,64},{64,7... | collective-permute-start | bytes 1544 | tf_op jit(solution)/shard_map/ppermute | solution.py:56
  183.6 11.3 %collective-permute-start.35 = (f32[1,8,16]{2,1,0:T(8,128)S(1)}, f32[1,8,16]{2,1,0:T(8,128)S(1)}, u32[]{:S(2)}, u32[]{:S(2)}) collective-permute-start(f32[1,8,16]{2,1,0:T(8,128)S(1)} %multiply_bitcast_fusion), channel_id=1, source_target_pairs={{8,0},{16,8},{24,16},{32,24},{40,32},{48,40},{56,48},{64,56},{72,6... | collective-permute-start | bytes 1544 | tf_op jit(solution)/shard_map/ppermute | solution.py:58
  215.3 10.5 %collective-permute-start.38 = (f32[1,8,16]{2,1,0:T(8,128)S(1)}, f32[1,8,16]{2,1,0:T(8,128)S(1)}, u32[]{:S(2)}, u32[]{:S(2)}) collective-permute-start(f32[1,8,16]{2,1,0:T(8,128)S(1)} %fusion.298), channel_id=1, source_target_pairs={{0,8},{8,16},{16,24},{24,32},{32,40},{40,48},{48,56},{56,64},{64,7... | collective-permute-start | bytes 1544 | tf_op jit(solution)/shard_map/ppermute | solution.py:56
  226.2 10.4 %collective-permute-start.40 = (f32[1,8,16]{2,1,0:T(8,128)S(1)}, f32[1,8,16]{2,1,0:T(8,128)S(1)}, u32[]{:S(2)}, u32[]{:S(2)}) collective-permute-start(f32[1,8,16]{2,1,0:T(8,128)S(1)} %fusion.289), channel_id=1, source_target_pairs={{0,8},{8,16},{16,24},{24,32},{32,40},{40,48},{48,56},{56,64},{64,7... | collective-permute-start | bytes 1544 | tf_op jit(solution)/shard_map/ppermute | solution.py:56
  237.5 12.9 %collective-permute-start.42 = (f32[1,16,32]{2,1,0:T(8,128)S(1)}, f32[1,16,32]{2,1,0:T(8,128)S(1)}, u32[]{:S(2)}, u32[]{:S(2)}) collective-permute-start(f32[1,16,32]{2,1,0:T(8,128)S(1)} %get-tuple-element.129), channel_id=1, source_target_pairs={{0,8},{8,16},{16,24},{24,32},{32,40},{40,48},{48,56},{56,64},{64,7... | collective-permute-start | bytes 6152 | tf_op jit(solution)/shard_map/ppermute | solution.py:56
  263.4 20.8 %collective-permute-start.48 = (f32[4,1,64]{2,1,0:T(1,128)S(1)}, f32[4,1,64]{2,1,0:T(1,128)S(1)}, u32[]{:S(2)}, u32[]{:S(2)}) collective-permute-start(f32[4,1,64]{2,1,0:T(1,128)S(1)} %get-tuple-element.164), channel_id=1, source_target_pairs={{0,1},{1,2},{2,3},{3,4},{4,5},{5,6},{6,7},{8,9},{9,10},{10,11},{11... | collective-permute-start | bytes 3080 | tf_op jit(solution)/shard_map/ppermute | solution.py:36
  265.3 18.9 %collective-permute-start.49 = (f32[4,1,64]{2,1,0:T(1,128)S(1)}, f32[4,1,64]{2,1,0:T(1,128)S(1)}, u32[]{:S(2)}, u32[]{:S(2)}) collective-permute-start(f32[4,1,64]{2,1,0:T(1,128)S(1)} %get-tuple-element.165), channel_id=1, source_target_pairs={{1,0},{2,1},{3,2},{4,3},{5,4},{6,5},{7,6},{9,8},{10,9},{11,10},{12... | collective-permute-start | bytes 3080 | tf_op jit(solution)/shard_map/ppermute | solution.py:37
  268.9 15.2 %collective-permute-start.46 = (f32[1,4,64]{2,1,0:T(4,128)S(1)}, f32[1,4,64]{2,1,0:T(4,128)S(1)}, u32[]{:S(2)}, u32[]{:S(2)}) collective-permute-start(f32[1,4,64]{2,1,0:T(4,128)S(1)} %get-tuple-element.162), channel_id=1, source_target_pairs={{0,8},{8,16},{16,24},{24,32},{32,40},{40,48},{48,56},{56,64},{64,7... | collective-permute-start | bytes 3080 | tf_op jit(solution)/shard_map/ppermute | solution.py:36
  284.4 21.9 %collective-permute-start.52 = (f32[4,1,64]{2,1,0:T(1,128)S(1)}, f32[4,1,64]{2,1,0:T(1,128)S(1)}, u32[]{:S(2)}, u32[]{:S(2)}) collective-permute-start(f32[4,1,64]{2,1,0:T(1,128)S(1)} %get-tuple-element.160), channel_id=1, source_target_pairs={{0,1},{1,2},{2,3},{3,4},{4,5},{5,6},{6,7},{8,9},{9,10},{10,11},{11... | collective-permute-start | bytes 3080 | tf_op jit(solution)/shard_map/ppermute | solution.py:36
  286.3 20.0 %collective-permute-start.53 = (f32[4,1,64]{2,1,0:T(1,128)S(1)}, f32[4,1,64]{2,1,0:T(1,128)S(1)}, u32[]{:S(2)}, u32[]{:S(2)}) collective-permute-start(f32[4,1,64]{2,1,0:T(1,128)S(1)} %get-tuple-element.161), channel_id=1, source_target_pairs={{1,0},{2,1},{3,2},{4,3},{5,4},{6,5},{7,6},{9,8},{10,9},{11,10},{12... | collective-permute-start | bytes 3080 | tf_op jit(solution)/shard_map/ppermute | solution.py:37
  290.0 16.4 %collective-permute-start.50 = (f32[1,4,64]{2,1,0:T(4,128)S(1)}, f32[1,4,64]{2,1,0:T(4,128)S(1)}, u32[]{:S(2)}, u32[]{:S(2)}) collective-permute-start(f32[1,4,64]{2,1,0:T(4,128)S(1)} %get-tuple-element.158), channel_id=1, source_target_pairs={{0,8},{8,16},{16,24},{24,32},{32,40},{40,48},{48,56},{56,64},{64,7... | collective-permute-start | bytes 3080 | tf_op jit(solution)/shard_map/ppermute | solution.py:36
  293.9 12.4 %collective-permute-start.51 = (f32[1,4,64]{2,1,0:T(4,128)S(1)}, f32[1,4,64]{2,1,0:T(4,128)S(1)}, u32[]{:S(2)}, u32[]{:S(2)}) collective-permute-start(f32[1,4,64]{2,1,0:T(4,128)S(1)} %get-tuple-element.159), channel_id=1, source_target_pairs={{8,0},{16,8},{24,16},{32,24},{40,32},{48,40},{56,48},{64,56},{72,6... | collective-permute-start | bytes 3080 | tf_op jit(solution)/shard_map/ppermute | solution.py:37
  307.0 13.1 %collective-permute-start.56 = (f32[8,1,128]{2,1,0:T(1,128)S(1)}, f32[8,1,128]{2,1,0:T(1,128)S(1)}, u32[]{:S(2)}, u32[]{:S(2)}) collective-permute-start(f32[8,1,128]{2,1,0:T(1,128)S(1)} %get-tuple-element.106), channel_id=1, source_target_pairs={{0,1},{1,2},{2,3},{3,4},{4,5},{5,6},{6,7},{8,9},{9,10},{10,11},{11... | collective-permute-start | bytes 12296 | tf_op jit(solution)/shard_map/ppermute | solution.py:36
  308.9 11.2 %collective-permute-start.57 = (f32[8,1,128]{2,1,0:T(1,128)S(1)}, f32[8,1,128]{2,1,0:T(1,128)S(1)}, u32[]{:S(2)}, u32[]{:S(2)}) collective-permute-start(f32[8,1,128]{2,1,0:T(1,128)S(1)} %get-tuple-element.107), channel_id=1, source_target_pairs={{1,0},{2,1},{3,2},{4,3},{5,4},{6,5},{7,6},{9,8},{10,9},{11,10},{12... | collective-permute-start | bytes 12296 | tf_op jit(solution)/shard_map/ppermute | solution.py:37
  326.9 15.1 %collective-permute-start.60 = (f32[8,1,128]{2,1,0:T(1,128)S(1)}, f32[8,1,128]{2,1,0:T(1,128)S(1)}, u32[]{:S(2)}, u32[]{:S(2)}) collective-permute-start(f32[8,1,128]{2,1,0:T(1,128)S(1)} %get-tuple-element.102), channel_id=1, source_target_pairs={{0,1},{1,2},{2,3},{3,4},{4,5},{5,6},{6,7},{8,9},{9,10},{10,11},{11... | collective-permute-start | bytes 12296 | tf_op jit(solution)/shard_map/ppermute | solution.py:36
  328.9 13.2 %collective-permute-start.61 = (f32[8,1,128]{2,1,0:T(1,128)S(1)}, f32[8,1,128]{2,1,0:T(1,128)S(1)}, u32[]{:S(2)}, u32[]{:S(2)}) collective-permute-start(f32[8,1,128]{2,1,0:T(1,128)S(1)} %get-tuple-element.103), channel_id=1, source_target_pairs={{1,0},{2,1},{3,2},{4,3},{5,4},{6,5},{7,6},{9,8},{10,9},{11,10},{12... | collective-permute-start | bytes 12296 | tf_op jit(solution)/shard_map/ppermute | solution.py:37
  345.6 28.6 %collective-permute-start.64 = (f32[8,1,128]{2,1,0:T(1,128)S(1)}, f32[8,1,128]{2,1,0:T(1,128)S(1)}, u32[]{:S(2)}, u32[]{:S(2)}) collective-permute-start(f32[8,1,128]{2,1,0:T(1,128)S(1)} %get-tuple-element.99), channel_id=1, source_target_pairs={{1,0},{2,1},{3,2},{4,3},{5,4},{6,5},{7,6},{9,8},{10,9},{11,10},{12... | collective-permute-start | bytes 12296 | tf_op jit(solution)/shard_map/ppermute | solution.py:37
  347.5 26.7 %collective-permute-start.65 = (f32[8,1,128]{2,1,0:T(1,128)S(1)}, f32[8,1,128]{2,1,0:T(1,128)S(1)}, u32[]{:S(2)}, u32[]{:S(2)}) collective-permute-start(f32[8,1,128]{2,1,0:T(1,128)S(1)} %get-tuple-element.98), channel_id=1, source_target_pairs={{0,1},{1,2},{2,3},{3,4},{4,5},{5,6},{6,7},{8,9},{9,10},{10,11},{11... | collective-permute-start | bytes 12296 | tf_op jit(solution)/shard_map/ppermute | solution.py:36
  349.9 24.3 %collective-permute-start.62 = (f32[1,8,128]{2,1,0:T(8,128)S(1)}, f32[1,8,128]{2,1,0:T(8,128)S(1)}, u32[]{:S(2)}, u32[]{:S(2)}) collective-permute-start(f32[1,8,128]{2,1,0:T(8,128)S(1)} %get-tuple-element.97), channel_id=1, source_target_pairs={{8,0},{16,8},{24,16},{32,24},{40,32},{48,40},{56,48},{64,56},{72,6... | collective-permute-start | bytes 12296 | tf_op jit(solution)/shard_map/ppermute | solution.py:37
  351.8 22.4 %collective-permute-start.63 = (f32[1,8,128]{2,1,0:T(8,128)S(1)}, f32[1,8,128]{2,1,0:T(8,128)S(1)}, u32[]{:S(2)}, u32[]{:S(2)}) collective-permute-start(f32[1,8,128]{2,1,0:T(8,128)S(1)} %get-tuple-element.96), channel_id=1, source_target_pairs={{0,8},{8,16},{16,24},{24,32},{32,40},{40,48},{48,56},{56,64},{64,7... | collective-permute-start | bytes 12296 | tf_op jit(solution)/shard_map/ppermute | solution.py:36
  383.4 16.4 %collective-permute-start.66 = (f32[3,384]{1,0:T(4,128)S(1)}, f32[3,384]{1,0:T(4,128)S(1)}, u32[]{:S(2)}, u32[]{:S(2)}) collective-permute-start(f32[3,384]{1,0:T(4,128)S(1)} %bitcast.273), channel_id=1, source_target_pairs={{0,16},{8,24},{16,32},{24,40},{32,48},{40,56},{48,64},{56,72},{64,... | collective-permute-start | bytes 13832 | tf_op jit(solution)/shard_map/ppermute | solution.py:68
  (32 other events, 817.2 us)
where the time goes:
time: 410 us; the launch traced here: 406 us
  starting transfers between devices  257 us (63%)
  local copies, waits for them, and re-layouts  55.8 us (14%)
  other arithmetic  47.2 us (12%)
  waiting for transfers between devices  41.9 us (10%)
    ppermute x22, starting transfers between devices, extended(): lax.ppermute(last, axis, up)  82.1 us
    ppermute x22, starting transfers between devices, extended(): lax.ppermute(initial, axis, [(b, a) for a, b in up])  60.9 us
    ppermute x9, starting transfers between devices, padded_2(): lax.ppermute(tail, axis, [(i, (i + 1) % count) for i in range(ends)])  54.8 us
    ppermute x8, starting transfers between devices, from_behind(): return lax.ppermute(block, axis, route)  31 us
    ppermute x22, waiting for transfers between devices, extended(): lax.ppermute(initial, axis, [(b, a) for a, b in up])  18.6 us
    ppermute x9, starting transfers between devices, padded_2(): lax.ppermute(head, axis, [((i + 1) % count, i) for i in range(ends)])  17.5 us
    ppermute x9, waiting for transfers between devices, padded_2(): lax.ppermute(head, axis, [((i + 1) % count, i) for i in range(ends)])  14.5 us
    scatter-add x1, other arithmetic, local(): jnp.zeros((3, total_cells), jnp.float32).at[:, where_in].add(-drag_force)  14.2 us
  transfers between devices with their start and end apart: 72, of which 11 were waited for; matrix products, arithmetic and copies ran while one was open for 17% of the time, Pallas kernels for 0%

commit v1 on v0

v1 whole, which is shorter than its diff:
```python
import functools

import jax
import jax.numpy as jnp
from jax import lax
from jax.experimental import pallas as pl
from jax.experimental.pallas import tpu as pltpu
from jax.sharding import PartitionSpec as P

SPREAD = 2
CAP = 3
GROUPS = 2 * SPREAD + 1
SLOTS = GROUPS * CAP
REACH = 7
RHS_REACH = 6

relax_weight = 0.8
solid_most = 0.6
void_power = 2.65
drag_base = 0.5
drag_slope = 0.5
stiffness = 16.0
softening = 0.1
particle_density = 2.0
step_duration = 0.25
gravity = -1.0

F32 = jnp.float32
BF16 = jnp.bfloat16
MESH = pl.DeviceIdType.MESH
AROUND = [(a, b) for a in (-1, 0, 1) for b in (-1, 0, 1) if (a, b) != (0, 0)]


def iota(shape, dim):
    return lax.broadcasted_iota(jnp.int32, shape, dim)


def zloop(low, high, body, step=4):
    whole = (high - low) // step
    if whole > 1:

        def chunk(i, carry):
            for k in range(step):
                body(low + i * step + k)
            return carry

        lax.fori_loop(0, whole, chunk, 0)
    else:
        whole = 0
    for z in range(low + whole * step, high):
        body(z)


def turn(v, shift, axis):
    return pltpu.roll(v, shift % v.shape[axis], axis)


def lanes_before(v, s):
    return jnp.where(iota(v.shape, 1) >= s, turn(v, s, 1), 0.0)


def lanes_after(v, s):
    return jnp.where(iota(v.shape, 1) < v.shape[1] - s, turn(v, -s, 1), 0.0)


def rows_before(v, s):
    return jnp.where(iota(v.shape, 0) >= s, turn(v, s, 0), 0.0)


def rows_after(v, s):
    return jnp.where(iota(v.shape, 0) < v.shape[0] - s, turn(v, -s, 0), 0.0)


def pair_sum(v, s, axis):
    low = (iota(v.shape, axis) & s) == 0
    return v + jnp.where(low, turn(v, -s, axis), turn(v, s, axis))


def halves(v):
    high = v.astype(BF16)
    return high, (v - high.astype(F32)).astype(BF16)


def kernel(
    nw, nn,
    counts, offs, nbr, pos, vel, rad, cell, gas, source, before,
    p_out, g_out, u_out,
    stage, pin, back, drg, gath, grow, con, cols,
    ohx, slhs, rlhs, glhs,
    por0, c0, b0, va0, vb0, z0, ym0, yp0, xm0, xp0, dg0, di0,
    por1, b1, va1, vb1, z1, ym1, yp1, xm1, xp1, dg1, di1,
    l1out, l1in, c1p, c1b, l2p, l2b,
    p2, b2, va2, vb2, z2, ci2, co2, xm2, xp2, dg2, di2,
    p3, b3, va3, vb3, z3, y3, xm3, xp3, dg3, di3,
    vfin,
    s_a, r_a, s_c0, r_c0, s_b, r_b, s_l1, r_l1, s_1p, r_1p, s_1b, r_1b, s_2p, r_2p, s_2b, r_2b, s_d, r_d,
):
    w = lax.axis_index("wide")
    n = lax.axis_index("narrow")
    blocks, slots = rad.shape

    def w_ok(d):
        return jnp.logical_and(w + d >= 0, w + d < nw)

    def n_ok(d):
        return jnp.logical_and(n + d >= 0, n + d < nn)

    def there(a, b):
        if b == 0:
            return w_ok(a)
        if a == 0:
            return n_ok(b)
        return jnp.logical_and(w_ok(a), n_ok(b))

    def remote(src, dst, send, recv, to):
        return pltpu.make_async_remote_copy(
            src_ref=src, dst_ref=dst, send_sem=send, recv_sem=recv, device_id=to, device_id_type=MESH
        )

    pending = []

    def start(copies):
        for copy, sends, _ in copies:
            pl.when(sends)(copy.start)
        pending.extend(copies)

    def arrive(copies):
        for copy, _, gets in copies:
            pl.when(gets)(copy.wait_recv)

    for ref in (pin, back, l1in, c1p, c1b, l2p, l2b, vfin):
        ref[...] = jnp.zeros_like(ref)
    for z in range(24):
        por0[z] = jnp.zeros((24, 128), F32)
        c0[z] = jnp.zeros((24, 128), F32)
    for z in range(8):
        c0[8 + z, 8:16] = source[z] + before[z] * (1.0 / step_duration)

    barrier = pltpu.get_barrier_semaphore()
    peers = []
    for d in range(1, REACH + 1):
        peers += [(w_ok(d), (w + d, n)), (w_ok(-d), (w - d, n))]
    for k in range(nn):
        peers.append((n != k, (w, k)))
    for a, b in AROUND:
        if a and b:
            peers.append((there(a, b), (w + a, n + b)))
    for ok, to in peers:
        pl.when(ok)(
            functools.partial(pl.semaphore_signal, barrier, inc=1, device_id=to, device_id_type=MESH)
        )

    off = [offs[b] for b in range(blocks)]
    rank = []
    for b in range(blocks):
        r = jnp.int32(0)
        for a in range(b):
            r = r + jnp.where(off[a] == off[b], 1, 0)
        rank.append(r)
    row8 = iota((blocks, slots), 0)
    live_count = jnp.zeros((blocks, slots), jnp.int32)
    for b in range(blocks):
        live_count = jnp.where(row8 == b, counts[b], live_count)
    live = jnp.where(iota((blocks, slots), 1) < live_count, 1.0, 0.0)
    radius = rad[...]
    volume = radius * radius * radius
    parts = [volume * live, vel[0], vel[1], vel[2], cell[...].astype(F32)]
    row16 = iota((16, slots), 0)
    for c, part in enumerate(parts):
        rows = jnp.zeros((16, slots), F32)
        for b in range(blocks):
            key = (off[b] + SPREAD) * CAP + rank[b]
            rows = jnp.where(row16 == key, jnp.broadcast_to(part[b : b + 1], rows.shape), rows)
        for o in range(GROUPS):
            stage[o, c * CAP : (c + 1) * CAP] = rows[o * CAP : (o + 1) * CAP]
    pin[SPREAD] = stage[SPREAD]

    count = jnp.int32(0)
    for ok, _ in peers:
        count = count + jnp.where(ok, 1, 0)
    pl.semaphore_wait(barrier, count)

    copies_a = []
    for o in range(GROUPS):
        d = o - SPREAD
        if d:
            copies_a.append(
                (remote(stage.at[o], pin.at[o], s_a.at[o], r_a.at[o], (w + d, n)), w_ok(d), w_ok(-d))
            )
    start(copies_a)

    def block_copies(ref, send, recv):
        return [
            (
                remote(
                    ref.at[8:16, 8:16],
                    ref.at[8 * (1 - a) : 8 * (2 - a), 8 * (1 - b) : 8 * (2 - b)],
                    send.at[i], recv.at[i], (w + a, n + b),
                ),
                there(a, b),
                there(-a, -b),
            )
            for i, (a, b) in enumerate(AROUND)
        ]

    copies_c0 = block_copies(c0, s_c0, r_c0)
    start(copies_c0)

    bar = jnp.concatenate(
        [pos[0], pos[1], pos[2], jnp.where(live > 0.0, radius, -1000.0), jnp.zeros((128 - 4 * blocks, slots), F32)],
        axis=0,
    ).T
    for c in range(4):
        for b in range(blocks):
            k = c * blocks + b
            cols[c, b] = jnp.broadcast_to(bar[:, k : k + 1], (slots, slots))
    factor = stiffness / (slots * 7)

    def contact_of(g, carry):
        own = [jnp.broadcast_to(pos[c, pl.ds(g, 1)], (8, slots)) for c in range(3)]
        own_rad = jnp.broadcast_to(rad[pl.ds(g, 1)], (8, slots))
        total = [jnp.zeros((8, slots), F32) for _ in range(3)]
        for k in range(7):
            other = g if k == 6 else nbr[g, k]
            for j in range(0, slots, 8):
                apart = [own[c] - cols[c, other, j : j + 8] for c in range(3)]
                square = apart[0] * apart[0] + apart[1] * apart[1]
                square = square + (apart[2] * apart[2] + softening * softening)
                inverse = lax.rsqrt(square)
                weight = jnp.maximum((own_rad + cols[3, other, j : j + 8]) * inverse - 1.0, 0.0)
                total = [total[c] + apart[c] * weight for c in range(3)]
        for c in range(3):
            con[c, pl.ds(g, 1)] = jnp.sum(total[c], axis=0, keepdims=True) * factor
        return carry

    lax.fori_loop(0, blocks, contact_of, 0)

    arrive(copies_a)

    zy_iota = iota((64, slots), 0)
    x_iota = iota((128, slots), 0)

    def cells_of(o, r):
        where = pin[o, 4 * CAP + r : 4 * CAP + r + 1].astype(jnp.int32)
        return where >> 7, where & 127

    def spread_volume(o, carry):
        for r in range(CAP):
            at = pl.ds(pl.multiple_of((o * CAP + r) * slots, slots), slots)
            zy, x = cells_of(o, r)
            one = jnp.where(jnp.broadcast_to(x, x_iota.shape) == x_iota, 1.0, 0.0).astype(BF16)
            ohx[0:128, at] = one
            ohx[128:256, at] = one
            hit = jnp.broadcast_to(zy, zy_iota.shape) == zy_iota
            here = jnp.where(hit, jnp.broadcast_to(pin[o, r : r + 1], zy_iota.shape), 0.0)
            high, low = halves(here)
            slhs[0:64, at] = high
            slhs[64:128, at] = low
        return carry

    lax.fori_loop(0, GROUPS, spread_volume, 0)
    both = lax.dot_general(
        slhs[...], ohx[0:128], (((1,), (1,)), ((), ())), preferred_element_type=F32
    )
    solid = both[0:64] + both[64:128]
    voidage = 1.0 - solid_most * solid / (1.0 + solid)
    for z in range(8):
        por0[8 + z, 8:16] = voidage[8 * z : 8 * z + 8]

    lane = iota((8, 128), 1)
    lane4 = iota((1, 128), 1) & 3

    def coarser(pairs, s):
        return pair_sum(pair_sum(pairs[0] + pairs[1], s, 0), s, 1) * 0.125

    def packed(cells):
        rows = [cells[0][0:1], cells[0][4:5], cells[1][0:1], cells[1][4:5]]
        row = rows[3]
        for k in range(3):
            row = jnp.where(lane4 == k, rows[k], row)
        return row

    finer = [coarser((voidage[16 * i : 16 * i + 8], voidage[16 * i + 8 : 16 * i + 16]), 1) for i in range(4)]
    c1p[n] = packed([coarser((finer[0], finer[1]), 2), coarser((finer[2], finer[3]), 2)])

    copies_b = block_copies(por0, s_b, r_b)
    start(copies_b)

    def row_copies(ref, send, recv):
        return [
            (
                remote(ref.at[n], ref.at[n], send.at[d], recv.at[d], (w, lax.rem(n + d, nn))),
                jnp.bool_(True),
                jnp.bool_(True),
            )
            for d in range(1, nn)
        ]

    def start_rows(copies):
        for copy, _, _ in copies:
            copy.start()
        pending.extend(copies)

    def arrive_rows(copies):
        for copy, _, _ in copies:
            copy.wait_recv()

    def slab_copies(ref, reach, send, recv):
        made = []
        for d in [s * k for k in range(1, reach + 1) for s in (1, -1)]:
            i = d + REACH
            made.append(
                (
                    remote(ref.at[REACH], ref.at[REACH - d], send.at[i], recv.at[i], (w + d, n)),
                    w_ok(d),
                    w_ok(-d),
                )
            )
        return made

    def rows_to_slab(ref):
        row = iota((8, 128), 0)
        slab = jnp.zeros((8, 128), F32)
        for k in range(nn):
            slab = jnp.where(row == k, jnp.broadcast_to(ref[k], (8, 128)), slab)
        return slab

    copies_1p = row_copies(c1p, s_1p, r_1p)
    start_rows(copies_1p)

    def fill_gather(f, values):
        high, low = halves(values)
        glhs[f * 64 : f * 64 + 64, 0:128] = high
        glhs[f * 64 : f * 64 + 64, 128:256] = low

    def gather(fields):
        def one(o, carry):
            for r in range(CAP):
                at = pl.ds(pl.multiple_of((o * CAP + r) * slots, slots), slots)
                found = jnp.dot(glhs[0 : 64 * fields], ohx[:, at], preferred_element_type=F32)
                zy, _ = cells_of(o, r)
                hit = jnp.broadcast_to(zy, zy_iota.shape) == zy_iota
                for f in range(fields):
                    gath[o, f * CAP + r : f * CAP + r + 1] = jnp.sum(
                        jnp.where(hit, found[64 * f : 64 * f + 64], 0.0), axis=0, keepdims=True
                    )
            return carry

        lax.fori_loop(0, GROUPS, one, 0)

    for f in range(3):
        fill_gather(f, gas[f].reshape(64, 128))
    fill_gather(3, voidage)
    gather(4)
    for o in range(GROUPS):
        slip = [gath[o, c * CAP : (c + 1) * CAP] - pin[o, (1 + c) * CAP : (2 + c) * CAP] for c in range(3)]
        speed = jnp.sqrt(slip[0] * slip[0] + slip[1] * slip[1] + slip[2] * slip[2])
        held = gath[o, 3 * CAP : 4 * CAP]
        scale = pin[o, 0:CAP] * (drag_base + drag_slope * speed) * jnp.exp(-void_power * jnp.log(held))
        for c in range(3):
            drg[o, c * CAP : (c + 1) * CAP] = scale * slip[c]

    arrive_rows(copies_1p)
    l2p[REACH] = rows_to_slab(c1p)
    copies_2p = slab_copies(l2p, REACH, s_2p, r_2p)
    start(copies_2p)

    def spread_drag(o, carry):
        for r in range(CAP):
            at = pl.ds(pl.multiple_of((o * CAP + r) * slots, slots), slots)
            zy, _ = cells_of(o, r)
            hit = jnp.broadcast_to(zy, zy_iota.shape) == zy_iota
            for c in range(3):
                row = drg[o, c * CAP + r : c * CAP + r + 1]
                high, low = halves(jnp.where(hit, jnp.broadcast_to(row, zy_iota.shape), 0.0))
                rlhs[128 * c : 128 * c + 64, at] = high
                rlhs[128 * c + 64 : 128 * c + 128, at] = low
        return carry

    lax.fori_loop(0, GROUPS, spread_drag, 0)
    sums = lax.dot_general(
        rlhs[...], ohx[0:128], (((1,), (1,)), ((), ())), preferred_element_type=F32
    )
    for c in range(3):
        onto = sums[128 * c : 128 * c + 64] + sums[128 * c + 64 : 128 * c + 128]
        grow[c] = gas[c].reshape(64, 128) - step_duration * onto / voidage

    arrive(copies_c0)
    arrive(copies_b)

    row24 = iota((24, 128), 0)
    inside_y = jnp.logical_and(
        jnp.logical_or(row24 >= 8, n > 0), jnp.logical_or(row24 < 16, n < nn - 1)
    )
    inside_y = jnp.where(inside_y, 1, 0)

    def inside(block):
        ok = jnp.logical_and(w + block >= 0, w + block < nw)
        return inside_y * jnp.where(ok, 1, 0) > 0

    def coefs(por, z, s, half, layers, cz, cym, cyp, cxm, cxp, dg, di):
        here = por[z]
        zm = half * (here + por[z - 1])
        zp = half * (here + por[z + 1])
        ym = half * (here + turn(here, s, 0))
        yp = half * (here + turn(here, -s, 0))
        xm = half * (here + lanes_before(here, s))
        xp = half * (here + lanes_after(here, s))
        diagonal = zm + zp + ym + yp + xm + xp
        lanes = iota(here.shape, 1)
        cz[z] = zm
        cym[z] = ym
        cyp[z] = yp
        cxm[z] = jnp.where(lanes >= s, xm, 0.0)
        cxp[z] = jnp.where(lanes < 128 - s, xp, 0.0)
        dg[z] = diagonal
        scaled = jnp.where(inside(z // layers - 1), relax_weight / diagonal, 0.0)
        di[z] = scaled
        return scaled

    def residual_at(v, b, z, s, cz, cym, cyp, cxm, cxp, dg):
        here = v[z]
        beside = cz[z] * v[z - 1] + cz[z + 1] * v[z + 1]
        beside = beside + (cym[z] * turn(here, s, 0) + cyp[z] * turn(here, -s, 0))
        beside = beside + (cxm[z] * turn(here, s, 1) + cxp[z] * turn(here, -s, 1))
        return here, (b[z] - dg[z] * here) + beside

    def sweep(v, to, b, z, s, cz, cym, cyp, cxm, cxp, dg, di):
        here, residual = residual_at(v, b, z, s, cz, cym, cyp, cxm, cxp, dg)
        to[z] = here + di[z] * residual

    level0 = (z0, ym0, yp0, xm0, xp0, dg0)
    level1 = (z1, ym1, yp1, xm1, xp1, dg1)

    def first0(z):
        b = c0[z] - por0[z] * (1.0 / step_duration)
        b0[z] = b
        va0[z] = coefs(por0, z, 1, 0.5, 8, *level0, di0) * b

    zloop(2, 22, first0)
    zloop(3, 21, lambda z: sweep(va0, vb0, b0, z, 1, *level0, di0))

    def por1_of(i):
        por1[i] = coarser((por0[2 * i], por0[2 * i + 1]), 1)

    zloop(0, 12, por1_of)

    def down0(i):
        _, low = residual_at(vb0, b0, 2 * i, 1, *level0)
        _, high = residual_at(vb0, b0, 2 * i + 1, 1, *level0)
        b1[i] = coarser((low, high), 1)

    zloop(2, 10, down0, 2)
    zloop(1, 11, lambda i: coefs(por1, i, 2, 0.125, 4, *level1, di1), 5)
    z1[11] = 0.125 * (por1[11] + por1[10])

    def first1(i):
        va1[i] = di1[i] * b1[i]

    zloop(2, 10, first1, 8)
    zloop(3, 9, lambda i: sweep(va1, vb1, b1, i, 2, *level1, di1), 6)
    left = [residual_at(vb1, b1, i, 2, *level1)[1][8:16] for i in range(4, 8)]
    c1b[n] = packed([coarser((left[0], left[1]), 2), coarser((left[2], left[3]), 2)])
    copies_1b = row_copies(c1b, s_1b, r_1b)
    start_rows(copies_1b)

    even_lane = (lane & 1) == 0
    row = iota((8, 128), 0)
    even_row = (row & 1) == 0
    for k in range(2):
        i = 4 + 2 * k
        right = jnp.where(even_lane, b1[i, 8:16], b1[i + 1, 8:16])
        iterate = jnp.where(even_lane, vb1[i, 8:16], vb1[i + 1, 8:16])
        l1out[k] = jnp.where(even_row, right, iterate)
    copies_l1 = [
        (
            remote(l1out, l1in.at[1 - a, 1 - b], s_l1.at[i], r_l1.at[i], (w + a, n + b)),
            there(a, b),
            there(-a, -b),
        )
        for i, (a, b) in enumerate(AROUND)
    ]
    start(copies_l1)

    arrive(copies_2p)

    def unpack4(slab):
        cells = []
        for k in range(4):
            one = jnp.where((lane & 3) == k, slab, 0.0)
            cells.append(pair_sum(pair_sum(one, 1, 1), 2, 1))
        return cells

    def unpack_por(k):
        cells = unpack4(l2p[k])
        for q in range(4):
            p2[2 * k + q // 2, q % 2] = cells[q]
        p3[k] = pair_sum((cells[0] + cells[1]) + (cells[2] + cells[3]), 4, 1) * 0.125

    zloop(0, 2 * REACH + 1, unpack_por, 5)
    real_row = jnp.where(row < nn, 1, 0)

    def inside_coarse(block):
        ok = jnp.logical_and(w + block >= 0, w + block < nw)
        return real_row * jnp.where(ok, 1, 0) > 0

    def coefs2(j):
        half = 0.5 * 0.25**2
        even, odd = p2[j, 0], p2[j, 1]
        inner = half * (even + odd)
        ci2[j] = inner
        outer = half * (even + rows_before(odd, 1))
        co2[j] = outer
        outer_odd = half * (odd + rows_after(even, 1))
        ok = inside_coarse(j // 2 - REACH)
        for y, here in enumerate((even, odd)):
            zm = half * (here + p2[j - 1, y])
            zp = half * (here + p2[j + 1, y])
            xm = half * (here + lanes_before(here, 4))
            xp = half * (here + lanes_after(here, 4))
            diagonal = zm + zp + inner + (outer_odd if y else outer) + xm + xp
            z2[j, y] = zm
            xm2[j, y] = jnp.where(lane >= 4, xm, 0.0)
            xp2[j, y] = jnp.where(lane < 124, xp, 0.0)
            dg2[j, y] = diagonal
            di2[j, y] = jnp.where(ok, relax_weight / diagonal, 0.0)

    zloop(1, 4 * REACH + 1, coefs2)

    def coefs3(k):
        half = 0.5 * 0.25**3
        here = p3[k]
        zm = half * (here + p3[k - 1])
        zp = half * (here + p3[k + 1])
        ym = half * (here + rows_before(here, 1))
        yp = half * (here + rows_after(here, 1))
        xm = half * (here + lanes_before(here, 8))
        xp = half * (here + lanes_after(here, 8))
        diagonal = zm + zp + ym + yp + xm + xp
        z3[k] = zm
        y3[k] = ym
        xm3[k] = jnp.where(lane >= 8, xm, 0.0)
        xp3[k] = jnp.where(lane < 120, xp, 0.0)
        dg3[k] = diagonal
        di3[k] = jnp.where(inside_coarse(k - REACH), relax_weight / diagonal, 0.0)

    zloop(1, 2 * REACH, coefs3)

    arrive_rows(copies_1b)
    l2b[REACH] = rows_to_slab(c1b)
    copies_2b = slab_copies(l2b, RHS_REACH, s_2b, r_2b)
    start(copies_2b)

    arrive(copies_l1)
    for a, b in AROUND:
        for k in range(2):
            both_layers = l1in[1 + a, 1 + b, k]
            for q in range(2):
                if q == 0:
                    layer = jnp.where(even_lane, both_layers, turn(both_layers, 1, 1))
                else:
                    layer = jnp.where(even_lane, turn(both_layers, -1, 1), both_layers)
                i = 4 * (1 + a) + 2 * k + q
                at = slice(8 * (1 + b), 8 * (2 + b))
                b1[i, at] = jnp.where(even_row, layer, turn(layer, 1, 0))
                vb1[i, at] = jnp.where(even_row, turn(layer, -1, 0), layer)

    def residual2(v, j):
        even, odd = v[j, 0], v[j, 1]
        outer = co2[j]
        made = []
        for y, here in enumerate((even, odd)):
            beside = z2[j, y] * v[j - 1, y] + z2[j + 1, y] * v[j + 1, y]
            if y == 0:
                beside = beside + (ci2[j] * odd + outer * rows_before(odd, 1))
            else:
                beside = beside + (ci2[j] * even + rows_after(outer, 1) * rows_after(even, 1))
            beside = beside + (xm2[j, y] * turn(here, 4, 1) + xp2[j, y] * turn(here, -4, 1))
            made.append((here, (b2[j, y] - dg2[j, y] * here) + beside))
        return made

    def sweep2(v, to):
        def at(j):
            for y, (here, residual) in enumerate(residual2(v, j)):
                to[j, y] = here + di2[j, y] * residual

        return at

    def residual3(v, k):
        here = v[k]
        beside = z3[k] * v[k - 1] + z3[k + 1] * v[k + 1]
        beside = beside + (y3[k] * rows_before(here, 1) + rows_after(y3[k], 1) * rows_after(here, 1))
        beside = beside + (xm3[k] * turn(here, 8, 1) + xp3[k] * turn(here, -8, 1))
        return here, (b3[k] - dg3[k] * here) + beside

    def sweep3(v, to):
        def at(k):
            here, residual = residual3(v, k)
            to[k] = here + di3[k] * residual

        return at

    arrive(copies_2b)

    def first2(k):
        cells = unpack4(l2b[k])
        for q in range(4):
            j, y = 2 * k + q // 2, q % 2
            b2[j, y] = cells[q]
            va2[j, y] = di2[j, y] * cells[q]

    zloop(1, 2 * REACH, first2)
    zloop(3, 27, sweep2(va2, vb2))

    def down2(k):
        low = residual2(vb2, 2 * k)
        high = residual2(vb2, 2 * k + 1)
        b = pair_sum((low[0][1] + low[1][1]) + (high[0][1] + high[1][1]), 4, 1) * 0.125
        b3[k] = b
        va3[k] = di3[k] * b

    zloop(2, 13, down2, 3)
    zloop(3, 12, sweep3(va3, vb3), 9)
    zloop(4, 11, sweep3(vb3, va3), 7)
    zloop(5, 10, sweep3(va3, vb3), 5)

    def up2(k):
        for q in range(4):
            j, y = 2 * k + q // 2, q % 2
            va2[j, y] = vb2[j, y] + vb3[k]

    zloop(5, 10, up2, 5)
    zloop(11, 19, sweep2(va2, vb2))
    for j in range(12, 18):
        for y, (here, residual) in enumerate(residual2(vb2, j)):
            vfin[j - 12, y, 8:16] = here + di2[j, y] * residual

    low_row = row < 4
    for q in range(6):
        for b in range(3):
            cells = [
                jnp.broadcast_to(vfin[q, y, pl.ds(7 + n + b, 1)], (8, 128)) for y in range(2)
            ]
            step = jnp.where(low_row, cells[0], cells[1])
            at = slice(8 * b, 8 * b + 8)
            for i in (2 * q, 2 * q + 1):
                va1[i, at] = vb1[i, at] + step
    zloop(1, 11, lambda i: sweep(va1, vb1, b1, i, 2, *level1, di1), 5)
    zloop(2, 10, lambda i: sweep(vb1, va1, b1, i, 2, *level1, di1))

    def up0(i):
        step = va1[i]
        va0[2 * i] = vb0[2 * i] + step
        va0[2 * i + 1] = vb0[2 * i + 1] + step

    zloop(2, 10, up0)
    zloop(6, 18, lambda z: sweep(va0, vb0, b0, z, 1, *level0, di0))
    zloop(7, 17, lambda z: sweep(vb0, va0, b0, z, 1, *level0, di0), 5)

    for z in range(8):
        whole = va0[8 + z]
        here = whole[8:16]
        p_out[z] = here
        slopes = [
            0.5 * (va0[9 + z, 8:16] - va0[7 + z, 8:16]),
            0.5 * (turn(whole, -1, 0)[8:16] - turn(whole, 1, 0)[8:16]),
            0.5 * (lanes_after(here, 1) - lanes_before(here, 1)),
        ]
        for c in range(3):
            g_out[c, z] = grow[c, 8 * z : 8 * z + 8] - step_duration * slopes[c]
            high, low = halves(slopes[c])
            glhs[64 * c + 8 * z : 64 * c + 8 * z + 8, 0:128] = high
            glhs[64 * c + 8 * z : 64 * c + 8 * z + 8, 128:256] = low
    gather(3)
    for o in range(GROUPS):
        for c in range(3):
            at = slice(c * CAP, (c + 1) * CAP)
            drg[o, at] = drg[o, at] - pin[o, 0:CAP] * gath[o, at]
    copies_d = []
    for o in range(GROUPS):
        d = o - SPREAD
        if d:
            copies_d.append(
                (remote(drg.at[o], back.at[o], s_d.at[o], r_d.at[o], (w - d, n)), w_ok(-d), w_ok(d))
            )
    start(copies_d)
    back[SPREAD] = drg[SPREAD]
    arrive(copies_d)
    for c in range(3):
        fluid = jnp.zeros((blocks, slots), F32)
        for b in range(blocks):
            one = back[off[b] + SPREAD, pl.ds(c * CAP + rank[b], 1)]
            fluid = jnp.where(row8 == b, jnp.broadcast_to(one, fluid.shape), fluid)
        push = (con[c] * live + fluid) / (particle_density * volume)
        if c == 0:
            push = push + gravity
        u_out[c] = live * (vel[c] + step_duration * push)

    for copy, sends, _ in pending:
        pl.when(sends)(copy.wait_send)


def local(nw, nn, position, velocity, radius, count, cell, offset, neighbours, gas, source, before):
    vmem = pl.BlockSpec(memory_space=pltpu.VMEM)
    smem = pl.BlockSpec(memory_space=pltpu.SMEM)

    def ram(*shape, dtype=F32):
        return pltpu.VMEM(shape, dtype)

    dma = pltpu.SemaphoreType.DMA
    block = ram(24, 24, 128)
    block1 = ram(12, 24, 128)
    tall = 2 * REACH + 1
    coarse2 = ram(2 * tall, 2, 8, 128)
    coarse2y = ram(2 * tall, 8, 128)
    coarse3 = ram(tall, 8, 128)
    particles = SLOTS * radius.shape[1]
    scratch = [
        *[ram(GROUPS, 16, 128)] * 5,
        ram(3, 64, 128),
        ram(3, 8, 128),
        ram(4, 8, 128, 128),
        ram(256, particles, dtype=BF16),
        ram(128, particles, dtype=BF16),
        ram(384, particles, dtype=BF16),
        ram(256, 256, dtype=BF16),
        *[block] * 12,
        *[block1] * 11,
        ram(2, 8, 128),
        ram(3, 3, 2, 8, 128),
        ram(8, 1, 128),
        ram(8, 1, 128),
        coarse3,
        coarse3,
        *[coarse2] * 5,
        coarse2y,
        coarse2y,
        *[coarse2] * 4,
        *[coarse3] * 10,
        ram(6, 2, 24, 128),
        *[dma((GROUPS,))] * 2,
        *[dma((8,))] * 6,
        *[dma((8,))] * 4,
        *[dma((tall,))] * 4,
        *[dma((GROUPS,))] * 2,
    ]
    return pl.pallas_call(
        functools.partial(kernel, nw, nn),
        out_shape=(
            jax.ShapeDtypeStruct(source.shape, F32),
            jax.ShapeDtypeStruct(gas.shape, F32),
            jax.ShapeDtypeStruct(velocity.shape, F32),
        ),
        in_specs=[smem] * 3 + [vmem] * 7,
        out_specs=(vmem, vmem, vmem),
        scratch_shapes=scratch,
        compiler_params=pltpu.CompilerParams(collective_id=0, has_side_effects=True),
        name="bed_step",
    )(count, offset, neighbours, position, velocity, radius, cell, gas, source, before)


def solution(mesh):
    placed = (
        P(None, ("wide", "narrow"), None),
        P(None, ("wide", "narrow"), None),
        P(("wide", "narrow"), None),
        P(("wide", "narrow")),
        P(("wide", "narrow"), None),
        P(("wide", "narrow")),
        P(("wide", "narrow"), None),
        P(None, "wide", "narrow", None),
        P("wide", "narrow", None),
        P("wide", "narrow", None),
    )
    return jax.shard_map(
        functools.partial(local, mesh.shape["wide"], mesh.shape["narrow"]),
        mesh=mesh,
        in_specs=placed,
        out_specs=(
            P("wide", "narrow", None),
            P(None, "wide", "narrow", None),
            P(None, ("wide", "narrow"), None),
        ),
        check_vma=False,
    )
```

time: 410 us -> 46.6 us (0.11)
  the two profiles are of different devices: /device:TPU:108 before, /device:TPU:96 now
where the time goes in v1:
time: 46.6 us; the launch traced here: 46.4 us
  Pallas kernels  42.2 us (91%)
  local copies, waits for them, and re-layouts  3.53 us (8%)
  between operations  0.64 us (1%)
    pallas_call x1, Pallas kernels, local(): pl.pallas_call(functools.partial(kernel, nw, nn), out_shape=(jax.ShapeDty...  42.2 us
    unnamed x5, local copies, waits for them, and re-layouts  3.53 us

profile of v1, /device:TPU:96, one launch (start us, length us, event | category | flops | bytes accessed | tf_op | source)
XLA Modules:
  0.0 46.4 jit_solution(6010515039470057431)
XLA Ops:
  0.6 42.2 %bed_step.1 = (f32[8,8,128]{2,1,0:T(8,128)}, f32[3,8,8,128]{3,2,1,0:T(8,128)}, f32[3,8,128]{2,1,0:T(8,128)}) custom-call(s32[8]{0:T(128)} %counts.1, s32[8]{0:T(128)} %offs.1, s32[8,6]{1,0:T(8,128)} %nbr.1, f32[3,8,128]{2,1,0:T(8,128)} %pos.1, f32[3,8,128]{2,1,0:T(8,128)} %vel.1, f32[8,128]{1,0:T(8,128)} %rad.1, s32[8,128]{1,0:T(8,128)} %cell.1, ...), custom_call_target="tpu_custom_call" | custom-call | tf_op jit(solution)/shard_map/bed_step/pallas_call | solution.py:747
  42.8 1.4 %copy.16 = f32[8,8,128]{2,1,0:T(8,128)} copy(f32[8,8,128]{2,1,0:T(8,128)} %get-tuple-element.6) | data formatting | bytes 65536
  44.2 0.0 copy-start
  44.2 1.6 %copy.17 = f32[3,8,8,128]{3,2,1,0:T(8,128)} copy(f32[3,8,8,128]{3,2,1,0:T(8,128)} %get-tuple-element.7) | data formatting | bytes 196608
  45.8 0.0 copy-done
  45.8 0.6 %copy.18 = f32[3,8,128]{2,1,0:T(8,128)} copy(f32[3,8,128]{2,1,0:T(8,128)S(1)} %copy-done) | data formatting | bytes 24576
Async XLA Ops:
  44.2 1.6 %copy-start = (f32[3,8,128]{2,1,0:T(8,128)S(1)}, f32[3,8,128]{2,1,0:T(8,128)}, u32[]{:S(2)}) copy-start(f32[3,8,128]{2,1,0:T(8,128)} %get-tuple-element.8) | copy-start | bytes 36868

commit v2 on v1

--- a/solution.py
+++ b/solution.py
@@ -83,10 +83,11 @@
 
 def kernel(
     nw, nn,
-    counts, offs, nbr, pos, vel, rad, cell, gas, source, before,
+    counts_in, offs_in, nbr_in, pos_in, vel_in, rad_in, cell_in, gas_in, source_in, before_in,
     p_out, g_out, u_out,
+    counts, offs, nbr, pos, vel, rad, cell, gas, source, before, s_in,
     stage, pin, back, drg, gath, grow, con, cols,
-    ohx, slhs, rlhs, glhs,
+    ohx, rlhs, glhs,
     por0, c0, b0, va0, vb0, z0, ym0, yp0, xm0, xp0, dg0, di0,
     por1, b1, va1, vb1, z1, ym1, yp1, xm1, xp1, dg1, di1,
     l1out, l1in, c1p, c1b, l2p, l2b,
@@ -128,14 +129,17 @@
         for copy, _, gets in copies:
             pl.when(gets)(copy.wait_recv)
 
+    given = (counts_in, offs_in, nbr_in, pos_in, vel_in, rad_in, cell_in, gas_in, source_in, before_in)
+    taken = (counts, offs, nbr, pos, vel, rad, cell, gas, source, before)
+    loads = [pltpu.make_async_copy(a, b, s_in.at[i]) for i, (a, b) in enumerate(zip(given, taken))]
+    for i in (0, 1, 5, 4, 6, 8, 9, 3, 2, 7):
+        loads[i].start()
+
     for ref in (pin, back, l1in, c1p, c1b, l2p, l2b, vfin):
         ref[...] = jnp.zeros_like(ref)
     for z in range(24):
         por0[z] = jnp.zeros((24, 128), F32)
         c0[z] = jnp.zeros((24, 128), F32)
-    for z in range(8):
-        c0[8 + z, 8:16] = source[z] + before[z] * (1.0 / step_duration)
-
     barrier = pltpu.get_barrier_semaphore()
     peers = []
     for d in range(1, REACH + 1):
@@ -149,6 +153,9 @@
         pl.when(ok)(
             functools.partial(pl.semaphore_signal, barrier, inc=1, device_id=to, device_id_type=MESH)
         )
+
+    for i in (0, 1, 5, 4, 6):
+        loads[i].wait()
 
     off = [offs[b] for b in range(blocks)]
     rank = []
@@ -174,6 +181,10 @@
         for o in range(GROUPS):
             stage[o, c * CAP : (c + 1) * CAP] = rows[o * CAP : (o + 1) * CAP]
     pin[SPREAD] = stage[SPREAD]
+    for i in (8, 9):
+        loads[i].wait()
+    for z in range(8):
+        c0[8 + z, 8:16] = source[z] + before[z] * (1.0 / step_duration)
 
     count = jnp.int32(0)
     for ok, _ in peers:
@@ -189,22 +200,31 @@
             )
     start(copies_a)
 
-    def block_copies(ref, send, recv):
-        return [
-            (
-                remote(
-                    ref.at[8:16, 8:16],
-                    ref.at[8 * (1 - a) : 8 * (2 - a), 8 * (1 - b) : 8 * (2 - b)],
-                    send.at[i], recv.at[i], (w + a, n + b),
-                ),
-                there(a, b),
-                there(-a, -b),
+    def block_copies(ref, corner, send, recv):
+        made = []
+        for i, (a, b) in enumerate(AROUND):
+            low, high = 8, 16
+            if a == 1:
+                low = 16 - corner[0 if b == 0 else 1]
+            if a == -1:
+                high = 8 + corner[0 if b == 0 else 1]
+            made.append(
+                (
+                    remote(
+                        ref.at[low:high, 8:16],
+                        ref.at[low - 8 * a : high - 8 * a, 8 * (1 - b) : 8 * (2 - b)],
+                        send.at[i], recv.at[i], (w + a, n + b),
+                    ),
+                    there(a, b),
+                    there(-a, -b),
+                )
             )
-            for i, (a, b) in enumerate(AROUND)
-        ]
-
-    copies_c0 = block_copies(c0, s_c0, r_c0)
-    start(copies_c0)
+        return made
+
+    copies_c0 = block_copies(c0, (6, 6), s_c0, r_c0)
+
+    for i in (3, 2, 7):
+        loads[i].wait()
 
     bar = jnp.concatenate(
         [pos[0], pos[1], pos[2], jnp.where(live > 0.0, radius, -1000.0), jnp.zeros((128 - 4 * blocks, slots), F32)],
@@ -233,7 +253,9 @@
             con[c, pl.ds(g, 1)] = jnp.sum(total[c], axis=0, keepdims=True) * factor
         return carry
 
-    lax.fori_loop(0, blocks, contact_of, 0)
+    lax.fori_loop(0, blocks // 2, contact_of, 0)
+    start(copies_c0)
+    lax.fori_loop(blocks // 2, blocks, contact_of, 0)
 
     arrive(copies_a)
 
@@ -244,28 +266,28 @@
         where = pin[o, 4 * CAP + r : 4 * CAP + r + 1].astype(jnp.int32)
         return where >> 7, where & 127
 
-    def spread_volume(o, carry):
+    both = jnp.zeros((128, 128), F32)
+    for o in range(GROUPS):
+        ones, values = [], []
         for r in range(CAP):
-            at = pl.ds(pl.multiple_of((o * CAP + r) * slots, slots), slots)
             zy, x = cells_of(o, r)
-            one = jnp.where(jnp.broadcast_to(x, x_iota.shape) == x_iota, 1.0, 0.0).astype(BF16)
-            ohx[0:128, at] = one
-            ohx[128:256, at] = one
+            ones.append(jnp.where(jnp.broadcast_to(x, x_iota.shape) == x_iota, 1.0, 0.0).astype(BF16))
             hit = jnp.broadcast_to(zy, zy_iota.shape) == zy_iota
             here = jnp.where(hit, jnp.broadcast_to(pin[o, r : r + 1], zy_iota.shape), 0.0)
-            high, low = halves(here)
-            slhs[0:64, at] = high
-            slhs[64:128, at] = low
-        return carry
-
-    lax.fori_loop(0, GROUPS, spread_volume, 0)
-    both = lax.dot_general(
-        slhs[...], ohx[0:128], (((1,), (1,)), ((), ())), preferred_element_type=F32
-    )
+            values.append(jnp.concatenate(halves(here), axis=0))
+        one = jnp.concatenate(ones, axis=1)
+        at = slice(o * CAP * slots, (o + 1) * CAP * slots)
+        ohx[0:128, at] = one
+        ohx[128:256, at] = one
+        both = both + lax.dot_general(
+            jnp.concatenate(values, axis=1), one, (((1,), (1,)), ((), ())), preferred_element_type=F32
+        )
     solid = both[0:64] + both[64:128]
     voidage = 1.0 - solid_most * solid / (1.0 + solid)
     for z in range(8):
         por0[8 + z, 8:16] = voidage[8 * z : 8 * z + 8]
+    copies_b = block_copies(por0, (8, 6), s_b, r_b)
+    start(copies_b)
 
     lane = iota((8, 128), 1)
     lane4 = iota((1, 128), 1) & 3
@@ -283,8 +305,6 @@
     finer = [coarser((voidage[16 * i : 16 * i + 8], voidage[16 * i + 8 : 16 * i + 16]), 1) for i in range(4)]
     c1p[n] = packed([coarser((finer[0], finer[1]), 2), coarser((finer[2], finer[3]), 2)])
 
-    copies_b = block_copies(por0, s_b, r_b)
-    start(copies_b)
 
     def row_copies(ref, send, recv):
         return [
@@ -335,14 +355,16 @@
 
     def gather(fields):
         def one(o, carry):
+            width = CAP * slots
+            at = pl.ds(pl.multiple_of(o * width, slots), width)
+            found = jnp.dot(glhs[0 : 64 * fields], ohx[:, at], preferred_element_type=F32)
             for r in range(CAP):
-                at = pl.ds(pl.multiple_of((o * CAP + r) * slots, slots), slots)
-                found = jnp.dot(glhs[0 : 64 * fields], ohx[:, at], preferred_element_type=F32)
                 zy, _ = cells_of(o, r)
                 hit = jnp.broadcast_to(zy, zy_iota.shape) == zy_iota
                 for f in range(fields):
                     gath[o, f * CAP + r : f * CAP + r + 1] = jnp.sum(
-                        jnp.where(hit, found[64 * f : 64 * f + 64], 0.0), axis=0, keepdims=True
+                        jnp.where(hit, found[64 * f : 64 * f + 64, r * slots : (r + 1) * slots], 0.0),
+                        axis=0, keepdims=True,
                     )
             return carry
 
@@ -660,14 +682,13 @@
     for z in range(8):
         whole = va0[8 + z]
         here = whole[8:16]
-        p_out[z] = here
         slopes = [
             0.5 * (va0[9 + z, 8:16] - va0[7 + z, 8:16]),
             0.5 * (turn(whole, -1, 0)[8:16] - turn(whole, 1, 0)[8:16]),
             0.5 * (lanes_after(here, 1) - lanes_before(here, 1)),
         ]
         for c in range(3):
-            g_out[c, z] = grow[c, 8 * z : 8 * z + 8] - step_duration * slopes[c]
+            g_out[c, z] = slopes[c]
             high, low = halves(slopes[c])
             glhs[64 * c + 8 * z : 64 * c + 8 * z + 8, 0:128] = high
             glhs[64 * c + 8 * z : 64 * c + 8 * z + 8, 128:256] = low
@@ -685,24 +706,38 @@
             )
     start(copies_d)
     back[SPREAD] = drg[SPREAD]
+    for z in range(8):
+        p_out[z] = va0[8 + z, 8:16]
+        for c in range(3):
+            g_out[c, z] = grow[c, 8 * z : 8 * z + 8] - step_duration * g_out[c, z]
+    for copy, sends, _ in pending[: -len(copies_d)]:
+        pl.when(sends)(copy.wait_send)
+    fluid_scale = live * step_duration / (particle_density * volume)
+    moved = [
+        live * (vel[c] + (step_duration * gravity if c == 0 else 0.0)) + fluid_scale * con[c] * live
+        for c in range(3)
+    ]
     arrive(copies_d)
     for c in range(3):
         fluid = jnp.zeros((blocks, slots), F32)
         for b in range(blocks):
             one = back[off[b] + SPREAD, pl.ds(c * CAP + rank[b], 1)]
             fluid = jnp.where(row8 == b, jnp.broadcast_to(one, fluid.shape), fluid)
-        push = (con[c] * live + fluid) / (particle_density * volume)
-        if c == 0:
-            push = push + gravity
-        u_out[c] = live * (vel[c] + step_duration * push)
-
-    for copy, sends, _ in pending:
+        u_out[c] = moved[c] + fluid_scale * fluid
+
+    for copy, sends, _ in copies_d:
         pl.when(sends)(copy.wait_send)
+
+
+def put_out(p, g, u, p_out, g_out, u_out):
+    p_out[...] = p[...]
+    g_out[...] = g[...]
+    u_out[...] = u[...]
 
 
 def local(nw, nn, position, velocity, radius, count, cell, offset, neighbours, gas, source, before):
     vmem = pl.BlockSpec(memory_space=pltpu.VMEM)
-    smem = pl.BlockSpec(memory_space=pltpu.SMEM)
+    hbm = pl.BlockSpec(memory_space=pltpu.HBM)
 
     def ram(*shape, dtype=F32):
         return pltpu.VMEM(shape, dtype)
@@ -715,13 +750,16 @@
     coarse2y = ram(2 * tall, 8, 128)
     coarse3 = ram(tall, 8, 128)
     particles = SLOTS * radius.shape[1]
+    given = (count, offset, neighbours, position, velocity, radius, cell, gas, source, before)
     scratch = [
+        *[pltpu.SMEM(a.shape, a.dtype) for a in given[:3]],
+        *[pltpu.VMEM(a.shape, a.dtype) for a in given[3:]],
+        dma((len(given),)),
         *[ram(GROUPS, 16, 128)] * 5,
         ram(3, 64, 128),
         ram(3, 8, 128),
         ram(4, 8, 128, 128),
         ram(256, particles, dtype=BF16),
-        ram(128, particles, dtype=BF16),
         ram(384, particles, dtype=BF16),
         ram(256, 256, dtype=BF16),
         *[block] * 12,
@@ -744,19 +782,30 @@
         *[dma((tall,))] * 4,
         *[dma((GROUPS,))] * 2,
     ]
-    return pl.pallas_call(
+    results = (
+        jax.ShapeDtypeStruct(source.shape, F32),
+        jax.ShapeDtypeStruct(gas.shape, F32),
+        jax.ShapeDtypeStruct(velocity.shape, F32),
+    )
+    made = pl.pallas_call(
         functools.partial(kernel, nw, nn),
-        out_shape=(
-            jax.ShapeDtypeStruct(source.shape, F32),
-            jax.ShapeDtypeStruct(gas.shape, F32),
-            jax.ShapeDtypeStruct(velocity.shape, F32),
-        ),
-        in_specs=[smem] * 3 + [vmem] * 7,
+        out_shape=results,
+        in_specs=[hbm] * len(given),
         out_specs=(vmem, vmem, vmem),
         scratch_shapes=scratch,
-        compiler_params=pltpu.CompilerParams(collective_id=0, has_side_effects=True),
+        compiler_params=pltpu.CompilerParams(
+            collective_id=0, has_side_effects=True, vmem_limit_bytes=24 << 20
+        ),
         name="bed_step",
-    )(count, offset, neighbours, position, velocity, radius, cell, gas, source, before)
+    )(*[pltpu.with_memory_space_constraint(a, pltpu.HBM) for a in given])
+    return pl.pallas_call(
+        put_out,
+        out_shape=results,
+        in_specs=[vmem] * 3,
+        out_specs=(vmem, vmem, vmem),
+        compiler_params=pltpu.CompilerParams(vmem_limit_bytes=8 << 20),
+        name="put_out",
+    )(*made)
 
 
 def solution(mesh):

time: 46.6 us -> 41.9 us (0.90)
  local copies, waits for them, and re-layouts: 3.53 us -> 0 us
  Pallas kernels: 42.2 us -> 41.1 us
    unnamed x5 -> x0, local copies, waits for them, and re-layouts: 3.53 us -> none
    pallas_call x1 -> x2, Pallas kernels: 42.2 us -> 41.1 us  [the longest x1 40.4 us: local(): pl.pallas_call(functools.partial(kernel, nw, nn), out_shape=results, in_s...]
where the time goes in v2:
time: 41.9 us; the launch traced here: 41.7 us
  Pallas kernels  41.1 us (98%)
  between operations  0.64 us (2%)
    pallas_call x1, Pallas kernels, local(): pl.pallas_call(functools.partial(kernel, nw, nn), out_shape=results, in_s...  40.4 us

profile of v2, /device:TPU:96, one launch (start us, length us, event | category | flops | bytes accessed | tf_op | source)
XLA Modules:
  0.0 41.7 jit_solution(7024289082998259850)
XLA Ops:
  0.6 40.4 %bed_step.1 = (f32[8,8,128]{2,1,0:T(8,128)S(1)}, f32[3,8,8,128]{3,2,1,0:T(8,128)S(1)}, f32[3,8,128]{2,1,0:T(8,128)S(1)}) custom-call(s32[8]{0:T(128)} %counts_in.1, s32[8]{0:T(128)} %offs_in.1, s32[8,6]{1,0:T(8,128)} %nbr_in.1, f32[3,8,128]{2,1,0:T(8,128)} %pos_in.1, f32[3,8,128]{2,1,0:T(8,128)} %vel_in.1, f32[8,128]{1,0:T(8,128)} %rad_in.1, ...), custom_call_target="tpu_custom_call" | custom-call | tf_op jit(solution)/shard_map/bed_step/pallas_call | solution.py:790
  41.1 0.7 %put_out.1 = (f32[8,8,128]{2,1,0:T(8,128)}, f32[3,8,8,128]{3,2,1,0:T(8,128)}, f32[3,8,128]{2,1,0:T(8,128)}) custom-call(f32[8,8,128]{2,1,0:T(8,128)S(1)} %get-tuple-element.6.p, f32[3,8,8,128]{3,2,1,0:T(8,128)S(1)} %get-tuple-element.7.g, f32[3,8,128]{2,1,0:T(8,128)S(1)} %get-tuple-element.8.u), custom_call_target="tpu_custom_call" | custom-call | tf_op jit(solution)/shard_map/put_out/pallas_call | solution.py:801

commit v3 on v2

--- a/solution.py
+++ b/solution.py
@@ -94,7 +94,7 @@
     p2, b2, va2, vb2, z2, ci2, co2, xm2, xp2, dg2, di2,
     p3, b3, va3, vb3, z3, y3, xm3, xp3, dg3, di3,
     vfin,
-    s_a, r_a, s_c0, r_c0, s_b, r_b, s_l1, r_l1, s_1p, r_1p, s_1b, r_1b, s_2p, r_2p, s_2b, r_2b, s_d, r_d,
+    s_a, r_a, s_c0, r_c0, s_b, r_b, s_l1, r_l1, s_1p, r_1p, s_1b, r_1b, s_2p, r_2p, s_2b, r_2b, s_d, r_d, hello,
 ):
     w = lax.axis_index("wide")
     n = lax.axis_index("narrow")
@@ -142,7 +142,7 @@
         c0[z] = jnp.zeros((24, 128), F32)
     barrier = pltpu.get_barrier_semaphore()
     peers = []
-    for d in range(1, REACH + 1):
+    for d in range(1, SPREAD + 1):
         peers += [(w_ok(d), (w + d, n)), (w_ok(-d), (w - d, n))]
     for k in range(nn):
         peers.append((n != k, (w, k)))
@@ -259,6 +259,13 @@
 
     arrive(copies_a)
 
+    for i, d in enumerate((2 * SPREAD, -2 * SPREAD)):
+        pl.when(w_ok(d))(
+            functools.partial(
+                pl.semaphore_signal, hello.at[i], inc=1, device_id=(w + d, n), device_id_type=MESH
+            )
+        )
+
     zy_iota = iota((64, slots), 0)
     x_iota = iota((128, slots), 0)
 
@@ -384,6 +391,8 @@
 
     arrive_rows(copies_1p)
     l2p[REACH] = rows_to_slab(c1p)
+    for i, d in enumerate((2 * SPREAD, -2 * SPREAD)):
+        pl.when(w_ok(-d))(functools.partial(pl.semaphore_wait, hello.at[i], 1))
     copies_2p = slab_copies(l2p, REACH, s_2p, r_2p)
     start(copies_2p)
 
@@ -781,6 +790,7 @@
         *[dma((8,))] * 4,
         *[dma((tall,))] * 4,
         *[dma((GROUPS,))] * 2,
+        pltpu.SemaphoreType.REGULAR((2,)),
     ]
     results = (
         jax.ShapeDtypeStruct(source.shape, F32),

time: 41.9 us -> 40.1 us (0.957)
  the two profiles are of different devices: /device:TPU:96 before, /device:TPU:102 now
where the time goes in v3:
time: 40.1 us; the launch traced here: 39.9 us
  Pallas kernels  39.3 us (98%)
  between operations  0.64 us (2%)
    pallas_call x1, Pallas kernels, local(): pl.pallas_call(functools.partial(kernel, nw, nn), out_shape=results, in_s...  38.6 us

profile of v3, /device:TPU:102, one launch (start us, length us, event | category | flops | bytes accessed | tf_op | source)
XLA Modules:
  0.0 39.9 jit_solution(12130911127397958537)
XLA Ops:
  0.6 38.6 %bed_step.1 = (f32[8,8,128]{2,1,0:T(8,128)S(1)}, f32[3,8,8,128]{3,2,1,0:T(8,128)S(1)}, f32[3,8,128]{2,1,0:T(8,128)S(1)}) custom-call(s32[8]{0:T(128)} %counts_in.1, s32[8]{0:T(128)} %offs_in.1, s32[8,6]{1,0:T(8,128)} %nbr_in.1, f32[3,8,128]{2,1,0:T(8,128)} %pos_in.1, f32[3,8,128]{2,1,0:T(8,128)} %vel_in.1, f32[8,128]{1,0:T(8,128)} %rad_in.1, ...), custom_call_target="tpu_custom_call" | custom-call | tf_op jit(solution)/shard_map/bed_step/pallas_call | solution.py:800
  39.3 0.7 %put_out.1 = (f32[8,8,128]{2,1,0:T(8,128)}, f32[3,8,8,128]{3,2,1,0:T(8,128)}, f32[3,8,128]{2,1,0:T(8,128)}) custom-call(f32[8,8,128]{2,1,0:T(8,128)S(1)} %get-tuple-element.6.p, f32[3,8,8,128]{3,2,1,0:T(8,128)S(1)} %get-tuple-element.7.g, f32[3,8,128]{2,1,0:T(8,128)S(1)} %get-tuple-element.8.u), custom_call_target="tpu_custom_call" | custom-call | tf_op jit(solution)/shard_map/put_out/pallas_call | solution.py:811

commit v4 on v3

--- a/solution.py
+++ b/solution.py
@@ -28,6 +28,7 @@
 F32 = jnp.float32
 BF16 = jnp.bfloat16
 MESH = pl.DeviceIdType.MESH
+EDGES = [(a, b) for a in (-1, 1) for b in (-1, 1)]
 AROUND = [(a, b) for a in (-1, 0, 1) for b in (-1, 0, 1) if (a, b) != (0, 0)]
 
 
@@ -90,7 +91,7 @@
     ohx, rlhs, glhs,
     por0, c0, b0, va0, vb0, z0, ym0, yp0, xm0, xp0, dg0, di0,
     por1, b1, va1, vb1, z1, ym1, yp1, xm1, xp1, dg1, di1,
-    l1out, l1in, c1p, c1b, l2p, l2b,
+    edge_out, edge_in, l1out, l1in, c1p, c1b, l2p, l2b,
     p2, b2, va2, vb2, z2, ci2, co2, xm2, xp2, dg2, di2,
     p3, b3, va3, vb3, z3, y3, xm3, xp3, dg3, di3,
     vfin,
@@ -135,7 +136,7 @@
     for i in (0, 1, 5, 4, 6, 8, 9, 3, 2, 7):
         loads[i].start()
 
-    for ref in (pin, back, l1in, c1p, c1b, l2p, l2b, vfin):
+    for ref in (pin, back, edge_in, l1in, c1p, c1b, l2p, l2b, vfin):
         ref[...] = jnp.zeros_like(ref)
     for z in range(24):
         por0[z] = jnp.zeros((24, 128), F32)
@@ -200,14 +201,16 @@
             )
     start(copies_a)
 
-    def block_copies(ref, corner, send, recv):
+    def block_copies(ref, layers, send, recv, corners=True):
         made = []
         for i, (a, b) in enumerate(AROUND):
+            if a and b and not corners:
+                continue
             low, high = 8, 16
             if a == 1:
-                low = 16 - corner[0 if b == 0 else 1]
+                low = 16 - layers
             if a == -1:
-                high = 8 + corner[0 if b == 0 else 1]
+                high = 8 + layers
             made.append(
                 (
                     remote(
@@ -221,7 +224,7 @@
             )
         return made
 
-    copies_c0 = block_copies(c0, (6, 6), s_c0, r_c0)
+    copies_c0 = block_copies(c0, 6, s_c0, r_c0)
 
     for i in (3, 2, 7):
         loads[i].wait()
@@ -293,8 +296,30 @@
     voidage = 1.0 - solid_most * solid / (1.0 + solid)
     for z in range(8):
         por0[8 + z, 8:16] = voidage[8 * z : 8 * z + 8]
-    copies_b = block_copies(por0, (8, 6), s_b, r_b)
+    copies_b = block_copies(por0, 8, s_b, r_b, corners=False)
     start(copies_b)
+
+    row = iota((8, 128), 0)
+    tiles = ((1, 6, 6), (2, 5, 6), (3, 4, 4))
+
+    def kept(b, rows):
+        return row >= 8 - rows if b == 1 else row < rows
+
+    copies_e = []
+    for e, (a, b) in enumerate(EDGES):
+        for k, (one, two, rows) in enumerate(tiles):
+            near, far = [por0[16 - d if a == 1 else 7 + d, 8:16] for d in (one, two)]
+            shift = 8 - rows if b == 1 else rows
+            edge_out[e, k] = jnp.where(kept(b, rows), near, turn(far, shift, 0))
+        i = AROUND.index((a, b))
+        copies_e.append(
+            (
+                remote(edge_out.at[e], edge_in.at[e], s_b.at[i], r_b.at[i], (w + a, n + b)),
+                there(a, b),
+                there(-a, -b),
+            )
+        )
+    start(copies_e)
 
     lane = iota((8, 128), 1)
     lane4 = iota((1, 128), 1) & 3
@@ -418,6 +443,14 @@
 
     arrive(copies_c0)
     arrive(copies_b)
+    arrive(copies_e)
+    for e, (a, b) in enumerate(EDGES):
+        for k, (one, two, rows) in enumerate(tiles):
+            tile = edge_in[e, k]
+            shift = 8 - rows if b == 1 else rows
+            at = slice(0, 8) if b == 1 else slice(16, 24)
+            for d, layer in ((one, tile), (two, turn(tile, -shift, 0))):
+                por0[8 - d if a == 1 else 15 + d, at] = layer
 
     row24 = iota((24, 128), 0)
     inside_y = jnp.logical_and(
@@ -516,11 +549,13 @@
     arrive(copies_2p)
 
     def unpack4(slab):
-        cells = []
-        for k in range(4):
-            one = jnp.where((lane & 3) == k, slab, 0.0)
-            cells.append(pair_sum(pair_sum(one, 1, 1), 2, 1))
-        return cells
+        def split(v, s):
+            low = (lane & s) == 0
+            return jnp.where(low, v, turn(v, s, 1)), jnp.where(low, turn(v, -s, 1), v)
+
+        first, second = split(slab, 1)
+        (zero, two), (one, three) = split(first, 2), split(second, 2)
+        return zero, one, two, three
 
     def unpack_por(k):
         cells = unpack4(l2p[k])
@@ -773,6 +808,8 @@
         ram(256, 256, dtype=BF16),
         *[block] * 12,
         *[block1] * 11,
+        ram(4, 3, 8, 128),
+        ram(4, 3, 8, 128),
         ram(2, 8, 128),
         ram(3, 3, 2, 8, 128),
         ram(8, 1, 128),

time: 40.1 us -> 39.8 us (level)
  no operation moved by 1% of the time
where the time goes in v4:
time: 39.8 us; the launch traced here: 39.6 us
  Pallas kernels  39 us (98%)
  between operations  0.64 us (2%)
    pallas_call x1, Pallas kernels, local(): pl.pallas_call(functools.partial(kernel, nw, nn), out_shape=results, in_s...  38.3 us

profile of v4, /device:TPU:102, one launch (start us, length us, event | category | flops | bytes accessed | tf_op | source)
XLA Modules:
  0.0 39.6 jit_solution(10338417112562931527)
XLA Ops:
  0.6 38.3 %bed_step.1 = (f32[8,8,128]{2,1,0:T(8,128)S(1)}, f32[3,8,8,128]{3,2,1,0:T(8,128)S(1)}, f32[3,8,128]{2,1,0:T(8,128)S(1)}) custom-call(s32[8]{0:T(128)} %counts_in.1, s32[8]{0:T(128)} %offs_in.1, s32[8,6]{1,0:T(8,128)} %nbr_in.1, f32[3,8,128]{2,1,0:T(8,128)} %pos_in.1, f32[3,8,128]{2,1,0:T(8,128)} %vel_in.1, f32[8,128]{1,0:T(8,128)} %rad_in.1, ...), custom_call_target="tpu_custom_call" | custom-call | tf_op jit(solution)/shard_map/bed_step/pallas_call | solution.py:837
  38.9 0.7 %put_out.1 = (f32[8,8,128]{2,1,0:T(8,128)}, f32[3,8,8,128]{3,2,1,0:T(8,128)}, f32[3,8,128]{2,1,0:T(8,128)}) custom-call(f32[8,8,128]{2,1,0:T(8,128)S(1)} %get-tuple-element.6.p, f32[3,8,8,128]{3,2,1,0:T(8,128)S(1)} %get-tuple-element.7.g, f32[3,8,128]{2,1,0:T(8,128)S(1)} %get-tuple-element.8.u), custom_call_target="tpu_custom_call" | custom-call | tf_op jit(solution)/shard_map/put_out/pallas_call | solution.py:848

commit v5 on v4

--- a/solution.py
+++ b/solution.py
@@ -86,7 +86,7 @@
     nw, nn,
     counts_in, offs_in, nbr_in, pos_in, vel_in, rad_in, cell_in, gas_in, source_in, before_in,
     p_out, g_out, u_out,
-    counts, offs, nbr, pos, vel, rad, cell, gas, source, before, s_in,
+    counts, offs, nbr, pos, vel, rad, cell, gas, source, before,
     stage, pin, back, drg, gath, grow, con, cols,
     ohx, rlhs, glhs,
     por0, c0, b0, va0, vb0, z0, ym0, yp0, xm0, xp0, dg0, di0,
@@ -95,7 +95,7 @@
     p2, b2, va2, vb2, z2, ci2, co2, xm2, xp2, dg2, di2,
     p3, b3, va3, vb3, z3, y3, xm3, xp3, dg3, di3,
     vfin,
-    s_a, r_a, s_c0, r_c0, s_b, r_b, s_l1, r_l1, s_1p, r_1p, s_1b, r_1b, s_2p, r_2p, s_2b, r_2b, s_d, r_d, hello,
+    sent, sent_b, sent_all, r_a, r_c0, r_b, r_l1, r_all, hello,
 ):
     w = lax.axis_index("wide")
     n = lax.axis_index("narrow")
@@ -119,12 +119,13 @@
             src_ref=src, dst_ref=dst, send_sem=send, recv_sem=recv, device_id=to, device_id_type=MESH
         )
 
-    pending = []
-
     def start(copies):
         for copy, sends, _ in copies:
             pl.when(sends)(copy.start)
-        pending.extend(copies)
+
+    def leave(copies):
+        for copy, sends, _ in copies:
+            pl.when(sends)(copy.wait_send)
 
     def arrive(copies):
         for copy, _, gets in copies:
@@ -132,7 +133,7 @@
 
     given = (counts_in, offs_in, nbr_in, pos_in, vel_in, rad_in, cell_in, gas_in, source_in, before_in)
     taken = (counts, offs, nbr, pos, vel, rad, cell, gas, source, before)
-    loads = [pltpu.make_async_copy(a, b, s_in.at[i]) for i, (a, b) in enumerate(zip(given, taken))]
+    loads = [pltpu.make_async_copy(a, b, sent.at[i]) for i, (a, b) in enumerate(zip(given, taken))]
     for i in (0, 1, 5, 4, 6, 8, 9, 3, 2, 7):
         loads[i].start()
 
@@ -196,9 +197,9 @@
     for o in range(GROUPS):
         d = o - SPREAD
         if d:
-            copies_a.append(
-                (remote(stage.at[o], pin.at[o], s_a.at[o], r_a.at[o], (w + d, n)), w_ok(d), w_ok(-d))
-            )
+            i = len(copies_a)
+            copy = remote(stage.at[o], pin.at[o], sent.at[(0, 1, 4, 5)[i]], r_a.at[i], (w + d, n))
+            copies_a.append((copy, w_ok(d), w_ok(-d)))
     start(copies_a)
 
     def block_copies(ref, layers, send, recv, corners=True):
@@ -216,7 +217,7 @@
                     remote(
                         ref.at[low:high, 8:16],
                         ref.at[low - 8 * a : high - 8 * a, 8 * (1 - b) : 8 * (2 - b)],
-                        send.at[i], recv.at[i], (w + a, n + b),
+                        send[i], recv.at[i], (w + a, n + b),
                     ),
                     there(a, b),
                     there(-a, -b),
@@ -224,7 +225,7 @@
             )
         return made
 
-    copies_c0 = block_copies(c0, 6, s_c0, r_c0)
+    copies_c0 = block_copies(c0, 6, [sent.at[i] for i in (2, 3, 6, 7, 8, 9, 10, 11)], r_c0)
 
     for i in (3, 2, 7):
         loads[i].wait()
@@ -288,7 +289,6 @@
         one = jnp.concatenate(ones, axis=1)
         at = slice(o * CAP * slots, (o + 1) * CAP * slots)
         ohx[0:128, at] = one
-        ohx[128:256, at] = one
         both = both + lax.dot_general(
             jnp.concatenate(values, axis=1), one, (((1,), (1,)), ((), ())), preferred_element_type=F32
         )
@@ -296,7 +296,7 @@
     voidage = 1.0 - solid_most * solid / (1.0 + solid)
     for z in range(8):
         por0[8 + z, 8:16] = voidage[8 * z : 8 * z + 8]
-    copies_b = block_copies(por0, 8, s_b, r_b, corners=False)
+    copies_b = block_copies(por0, 8, [sent_b.at[i] for i in range(8)], r_b, corners=False)
     start(copies_b)
 
     row = iota((8, 128), 0)
@@ -314,7 +314,7 @@
         i = AROUND.index((a, b))
         copies_e.append(
             (
-                remote(edge_out.at[e], edge_in.at[e], s_b.at[i], r_b.at[i], (w + a, n + b)),
+                remote(edge_out.at[e], edge_in.at[e], sent_b.at[i], r_b.at[i], (w + a, n + b)),
                 there(a, b),
                 there(-a, -b),
             )
@@ -338,37 +338,29 @@
     c1p[n] = packed([coarser((finer[0], finer[1]), 2), coarser((finer[2], finer[3]), 2)])
 
 
-    def row_copies(ref, send, recv):
-        return [
-            (
-                remote(ref.at[n], ref.at[n], send.at[d], recv.at[d], (w, lax.rem(n + d, nn))),
-                jnp.bool_(True),
-                jnp.bool_(True),
-            )
-            for d in range(1, nn)
-        ]
-
-    def start_rows(copies):
-        for copy, _, _ in copies:
-            copy.start()
-        pending.extend(copies)
-
-    def arrive_rows(copies):
-        for copy, _, _ in copies:
-            copy.wait_recv()
-
-    def slab_copies(ref, reach, send, recv):
-        made = []
+    def send_rows(ref, k):
+        for d in range(1, nn):
+            to = (w, lax.rem(n + d, nn))
+            remote(ref.at[n], ref.at[n], sent_all.at[k], r_all.at[k], to).start()
+
+    def all_rows(ref, k):
+        part = ref.at[0 : nn - 1]
+        return remote(part, part, sent_all.at[k], r_all.at[k], (w, lax.rem(n + 1, nn)))
+
+    def send_slab(ref, reach, k):
         for d in [s * k for k in range(1, reach + 1) for s in (1, -1)]:
-            i = d + REACH
-            made.append(
-                (
-                    remote(ref.at[REACH], ref.at[REACH - d], send.at[i], recv.at[i], (w + d, n)),
-                    w_ok(d),
-                    w_ok(-d),
-                )
-            )
-        return made
+            copy = remote(ref.at[REACH], ref.at[REACH - d], sent_all.at[k], r_all.at[k], (w + d, n))
+            pl.when(w_ok(d))(copy.start)
+
+    def all_slabs(ref, reach, k):
+        partners = jnp.int32(0)
+        for d in range(1, reach + 1):
+            partners = partners + jnp.where(w_ok(d), 1, 0) + jnp.where(w_ok(-d), 1, 0)
+        waits = []
+        for c in range(1, 2 * reach + 1):
+            part = ref.at[0:c]
+            waits.append((partners == c, remote(part, part, sent_all.at[k], r_all.at[k], (w, lax.rem(n + 1, nn)))))
+        return waits
 
     def rows_to_slab(ref):
         row = iota((8, 128), 0)
@@ -377,8 +369,9 @@
             slab = jnp.where(row == k, jnp.broadcast_to(ref[k], (8, 128)), slab)
         return slab
 
-    copies_1p = row_copies(c1p, s_1p, r_1p)
-    start_rows(copies_1p)
+    send_rows(c1p, 0)
+    for k in (slice(0, 64), slice(64, 128)):
+        ohx[128 + k.start : 128 + k.stop] = ohx[k]
 
     def fill_gather(f, values):
         high, low = halves(values)
@@ -414,12 +407,11 @@
         for c in range(3):
             drg[o, c * CAP : (c + 1) * CAP] = scale * slip[c]
 
-    arrive_rows(copies_1p)
+    all_rows(c1p, 0).wait_recv()
     l2p[REACH] = rows_to_slab(c1p)
     for i, d in enumerate((2 * SPREAD, -2 * SPREAD)):
         pl.when(w_ok(-d))(functools.partial(pl.semaphore_wait, hello.at[i], 1))
-    copies_2p = slab_copies(l2p, REACH, s_2p, r_2p)
-    start(copies_2p)
+    send_slab(l2p, REACH, 1)
 
     def spread_drag(o, carry):
         for r in range(CAP):
@@ -525,8 +517,8 @@
     zloop(3, 9, lambda i: sweep(va1, vb1, b1, i, 2, *level1, di1), 6)
     left = [residual_at(vb1, b1, i, 2, *level1)[1][8:16] for i in range(4, 8)]
     c1b[n] = packed([coarser((left[0], left[1]), 2), coarser((left[2], left[3]), 2)])
-    copies_1b = row_copies(c1b, s_1b, r_1b)
-    start_rows(copies_1b)
+    send_rows(c1b, 2)
+    leave(copies_a + copies_c0)
 
     even_lane = (lane & 1) == 0
     row = iota((8, 128), 0)
@@ -538,7 +530,7 @@
         l1out[k] = jnp.where(even_row, right, iterate)
     copies_l1 = [
         (
-            remote(l1out, l1in.at[1 - a, 1 - b], s_l1.at[i], r_l1.at[i], (w + a, n + b)),
+            remote(l1out, l1in.at[1 - a, 1 - b], sent.at[i], r_l1.at[i], (w + a, n + b)),
             there(a, b),
             there(-a, -b),
         )
@@ -546,7 +538,8 @@
     ]
     start(copies_l1)
 
-    arrive(copies_2p)
+    for ok, wait in all_slabs(l2p, REACH, 1):
+        pl.when(ok)(wait.wait_recv)
 
     def unpack4(slab):
         def split(v, s):
@@ -612,10 +605,10 @@
 
     zloop(1, 2 * REACH, coefs3)
 
-    arrive_rows(copies_1b)
+    all_rows(c1b, 2).wait_recv()
     l2b[REACH] = rows_to_slab(c1b)
-    copies_2b = slab_copies(l2b, RHS_REACH, s_2b, r_2b)
-    start(copies_2b)
+    send_slab(l2b, RHS_REACH, 3)
+    leave(copies_b + copies_e)
 
     arrive(copies_l1)
     for a, b in AROUND:
@@ -666,7 +659,8 @@
 
         return at
 
-    arrive(copies_2b)
+    for ok, wait in all_slabs(l2b, RHS_REACH, 3):
+        pl.when(ok)(wait.wait_recv)
 
     def first2(k):
         cells = unpack4(l2b[k])
@@ -745,8 +739,9 @@
     for o in range(GROUPS):
         d = o - SPREAD
         if d:
+            i = len(copies_d)
             copies_d.append(
-                (remote(drg.at[o], back.at[o], s_d.at[o], r_d.at[o], (w - d, n)), w_ok(-d), w_ok(d))
+                (remote(drg.at[o], back.at[o], sent_b.at[i], r_b.at[i], (w - d, n)), w_ok(-d), w_ok(d))
             )
     start(copies_d)
     back[SPREAD] = drg[SPREAD]
@@ -754,8 +749,11 @@
         p_out[z] = va0[8 + z, 8:16]
         for c in range(3):
             g_out[c, z] = grow[c, 8 * z : 8 * z + 8] - step_duration * g_out[c, z]
-    for copy, sends, _ in pending[: -len(copies_d)]:
-        pl.when(sends)(copy.wait_send)
+    leave(copies_l1)
+    all_rows(c1p, 0).wait_send()
+    all_rows(c1b, 2).wait_send()
+    for ok, wait in all_slabs(l2p, REACH, 1) + all_slabs(l2b, RHS_REACH, 3):
+        pl.when(ok)(wait.wait_send)
     fluid_scale = live * step_duration / (particle_density * volume)
     moved = [
         live * (vel[c] + (step_duration * gravity if c == 0 else 0.0)) + fluid_scale * con[c] * live
@@ -769,8 +767,7 @@
             fluid = jnp.where(row8 == b, jnp.broadcast_to(one, fluid.shape), fluid)
         u_out[c] = moved[c] + fluid_scale * fluid
 
-    for copy, sends, _ in copies_d:
-        pl.when(sends)(copy.wait_send)
+    leave(copies_d)
 
 
 def put_out(p, g, u, p_out, g_out, u_out):
@@ -798,7 +795,6 @@
     scratch = [
         *[pltpu.SMEM(a.shape, a.dtype) for a in given[:3]],
         *[pltpu.VMEM(a.shape, a.dtype) for a in given[3:]],
-        dma((len(given),)),
         *[ram(GROUPS, 16, 128)] * 5,
         ram(3, 64, 128),
         ram(3, 8, 128),
@@ -822,11 +818,12 @@
         *[coarse2] * 4,
         *[coarse3] * 10,
         ram(6, 2, 24, 128),
-        *[dma((GROUPS,))] * 2,
-        *[dma((8,))] * 6,
-        *[dma((8,))] * 4,
-        *[dma((tall,))] * 4,
-        *[dma((GROUPS,))] * 2,
+        dma((12,)),
+        dma((8,)),
+        dma((4,)),
+        dma((4,)),
+        *[dma((8,))] * 3,
+        dma((4,)),
         pltpu.SemaphoreType.REGULAR((2,)),
     ]
     results = (

time: 39.8 us -> 38.7 us (0.972)
  Pallas kernels: 39 us -> 37.9 us
    pallas_call x1, Pallas kernels: 38.3 us -> 37.2 us  [local(): pl.pallas_call(functools.partial(kernel, nw, nn), out_shape=results, in_s...]
where the time goes in v5:
time: 38.7 us; the launch traced here: 38.5 us
  Pallas kernels  37.9 us (98%)
  between operations  0.64 us (2%)
    pallas_call x1, Pallas kernels, local(): pl.pallas_call(functools.partial(kernel, nw, nn), out_shape=results, in_s...  37.2 us

profile of v5, /device:TPU:102, one launch (start us, length us, event | category | flops | bytes accessed | tf_op | source)
XLA Modules:
  0.0 38.5 jit_solution(11854714062993314407)
XLA Ops:
  0.6 37.2 %bed_step.1 = (f32[8,8,128]{2,1,0:T(8,128)S(1)}, f32[3,8,8,128]{3,2,1,0:T(8,128)S(1)}, f32[3,8,128]{2,1,0:T(8,128)S(1)}) custom-call(s32[8]{0:T(128)} %counts_in.1, s32[8]{0:T(128)} %offs_in.1, s32[8,6]{1,0:T(8,128)} %nbr_in.1, f32[3,8,128]{2,1,0:T(8,128)} %pos_in.1, f32[3,8,128]{2,1,0:T(8,128)} %vel_in.1, f32[8,128]{1,0:T(8,128)} %rad_in.1, ...), custom_call_target="tpu_custom_call" | custom-call | tf_op jit(solution)/shard_map/bed_step/pallas_call | solution.py:834
  37.9 0.7 %put_out.1 = (f32[8,8,128]{2,1,0:T(8,128)}, f32[3,8,8,128]{3,2,1,0:T(8,128)}, f32[3,8,128]{2,1,0:T(8,128)}) custom-call(f32[8,8,128]{2,1,0:T(8,128)S(1)} %get-tuple-element.6.p, f32[3,8,8,128]{3,2,1,0:T(8,128)S(1)} %get-tuple-element.7.g, f32[3,8,128]{2,1,0:T(8,128)S(1)} %get-tuple-element.8.u), custom_call_target="tpu_custom_call" | custom-call | tf_op jit(solution)/shard_map/put_out/pallas_call | solution.py:845

commit v6 on v5

--- a/solution.py
+++ b/solution.py
@@ -493,21 +493,21 @@
         b0[z] = b
         va0[z] = coefs(por0, z, 1, 0.5, 8, *level0, di0) * b
 
-    zloop(2, 22, first0)
-    zloop(3, 21, lambda z: sweep(va0, vb0, b0, z, 1, *level0, di0))
+    zloop(2, 22, first0, 20)
+    zloop(3, 21, lambda z: sweep(va0, vb0, b0, z, 1, *level0, di0), 18)
 
     def por1_of(i):
         por1[i] = coarser((por0[2 * i], por0[2 * i + 1]), 1)
 
-    zloop(0, 12, por1_of)
+    zloop(0, 12, por1_of, 12)
 
     def down0(i):
         _, low = residual_at(vb0, b0, 2 * i, 1, *level0)
         _, high = residual_at(vb0, b0, 2 * i + 1, 1, *level0)
         b1[i] = coarser((low, high), 1)
 
-    zloop(2, 10, down0, 2)
-    zloop(1, 11, lambda i: coefs(por1, i, 2, 0.125, 4, *level1, di1), 5)
+    zloop(2, 10, down0, 8)
+    zloop(1, 11, lambda i: coefs(por1, i, 2, 0.125, 4, *level1, di1), 10)
     z1[11] = 0.125 * (por1[11] + por1[10])
 
     def first1(i):
@@ -669,8 +669,8 @@
             b2[j, y] = cells[q]
             va2[j, y] = di2[j, y] * cells[q]
 
-    zloop(1, 2 * REACH, first2)
-    zloop(3, 27, sweep2(va2, vb2))
+    zloop(1, 2 * REACH, first2, 13)
+    zloop(3, 27, sweep2(va2, vb2), 24)
 
     def down2(k):
         low = residual2(vb2, 2 * k)
@@ -679,7 +679,7 @@
         b3[k] = b
         va3[k] = di3[k] * b
 
-    zloop(2, 13, down2, 3)
+    zloop(2, 13, down2, 11)
     zloop(3, 12, sweep3(va3, vb3), 9)
     zloop(4, 11, sweep3(vb3, va3), 7)
     zloop(5, 10, sweep3(va3, vb3), 5)
@@ -690,7 +690,7 @@
             va2[j, y] = vb2[j, y] + vb3[k]
 
     zloop(5, 10, up2, 5)
-    zloop(11, 19, sweep2(va2, vb2))
+    zloop(11, 19, sweep2(va2, vb2), 8)
     for j in range(12, 18):
         for y, (here, residual) in enumerate(residual2(vb2, j)):
             vfin[j - 12, y, 8:16] = here + di2[j, y] * residual
@@ -705,17 +705,17 @@
             at = slice(8 * b, 8 * b + 8)
             for i in (2 * q, 2 * q + 1):
                 va1[i, at] = vb1[i, at] + step
-    zloop(1, 11, lambda i: sweep(va1, vb1, b1, i, 2, *level1, di1), 5)
-    zloop(2, 10, lambda i: sweep(vb1, va1, b1, i, 2, *level1, di1))
+    zloop(1, 11, lambda i: sweep(va1, vb1, b1, i, 2, *level1, di1), 10)
+    zloop(2, 10, lambda i: sweep(vb1, va1, b1, i, 2, *level1, di1), 8)
 
     def up0(i):
         step = va1[i]
         va0[2 * i] = vb0[2 * i] + step
         va0[2 * i + 1] = vb0[2 * i + 1] + step
 
-    zloop(2, 10, up0)
-    zloop(6, 18, lambda z: sweep(va0, vb0, b0, z, 1, *level0, di0))
-    zloop(7, 17, lambda z: sweep(vb0, va0, b0, z, 1, *level0, di0), 5)
+    zloop(2, 10, up0, 8)
+    zloop(6, 18, lambda z: sweep(va0, vb0, b0, z, 1, *level0, di0), 12)
+    zloop(7, 17, lambda z: sweep(vb0, va0, b0, z, 1, *level0, di0), 10)
 
     for z in range(8):
         whole = va0[8 + z]

time: 38.7 us -> 36.8 us (0.951)
  Pallas kernels: 37.9 us -> 36 us
    pallas_call x1, Pallas kernels: 37.2 us -> 35.4 us  [local(): pl.pallas_call(functools.partial(kernel, nw, nn), out_shape=results, in_s...]
where the time goes in v6:
time: 36.8 us; the launch traced here: 36.7 us
  Pallas kernels  36 us (98%)
  between operations  0.64 us (2%)
    pallas_call x1, Pallas kernels, local(): pl.pallas_call(functools.partial(kernel, nw, nn), out_shape=results, in_s...  35.4 us

profile of v6, /device:TPU:102, one launch (start us, length us, event | category | flops | bytes accessed | tf_op | source)
XLA Modules:
  0.0 36.7 jit_solution(9296612355160504588)
XLA Ops:
  0.6 35.4 %bed_step.1 = (f32[8,8,128]{2,1,0:T(8,128)S(1)}, f32[3,8,8,128]{3,2,1,0:T(8,128)S(1)}, f32[3,8,128]{2,1,0:T(8,128)S(1)}) custom-call(s32[8]{0:T(128)} %counts_in.1, s32[8]{0:T(128)} %offs_in.1, s32[8,6]{1,0:T(8,128)} %nbr_in.1, f32[3,8,128]{2,1,0:T(8,128)} %pos_in.1, f32[3,8,128]{2,1,0:T(8,128)} %vel_in.1, f32[8,128]{1,0:T(8,128)} %rad_in.1, ...), custom_call_target="tpu_custom_call" | custom-call | tf_op jit(solution)/shard_map/bed_step/pallas_call | solution.py:834
  36.0 0.7 %put_out.1 = (f32[8,8,128]{2,1,0:T(8,128)}, f32[3,8,8,128]{3,2,1,0:T(8,128)}, f32[3,8,128]{2,1,0:T(8,128)}) custom-call(f32[8,8,128]{2,1,0:T(8,128)S(1)} %get-tuple-element.6.p, f32[3,8,8,128]{3,2,1,0:T(8,128)S(1)} %get-tuple-element.7.g, f32[3,8,128]{2,1,0:T(8,128)S(1)} %get-tuple-element.8.u), custom_call_target="tpu_custom_call" | custom-call | tf_op jit(solution)/shard_map/put_out/pallas_call | solution.py:845
